TPU v7x, 32 devices: a whole 2x2x4 slice. The times are simulated.
32 devices in a mesh: clump: 8 (over z, y), grp: 4 (over x, core).
Axes of the slice: x: 2, y: 2, z: 4, core: 2. Of those that a mesh axis runs over, the one named last changes fastest.
Arguments:
- flux: float32 [32, 1024, 64], P(('clump', 'grp')), may hold values from -6 to 6
- patch_pft: int32 [32, 1024], P(('clump', 'grp')), may hold values from 0 to 15
- patch_wt: float32 [32, 1024], P(('clump', 'grp')), may hold values from 0.2 to 2
- patch_col: int32 [32, 1024], P(('clump', 'grp')), may hold values from 0 to 511, never falling along the last dimension, each value on 1 to 4 neighbouring positions
- col_wt: float32 [32, 512], P(('clump', 'grp')), may hold values from 0.2 to 2
- col_lu: int32 [32, 512], P(('clump', 'grp')), may hold values from 0 to 255, never falling along the last dimension, each value on 1 to 4 neighbouring positions
- lu_wt: float32 [32, 256], P(('clump', 'grp')), may hold values from 0.2 to 2
- lu_grid: int32 [32, 256], P(('clump', 'grp')), may hold values from 0 to 127, never falling along the last dimension, each value on 1 to 4 neighbouring positions
- cell_target: int32 [32, 128], P(('clump', 'grp')), may hold values from 0 to 4095, as said below
- patch_count: int32 [32], P(('clump', 'grp')), may hold values from 64 to 1024
- pft_scale: float32 [16, 64], replicated, may hold values from 0.3 to 3
- cpl_frac: float32 [4096], P(('clump', 'grp')), may hold values from 0.2 to 0.9
- cpl_field: float32 [4096, 64], P(('clump', 'grp')), may hold values from -6 to 6
Outputs:
- grid_merged: float32 [4096, 64], P(('clump', 'grp'))
- anomaly: float32 [32, 1024, 64], P(('clump', 'grp'))
Inputs may be any that keep to these rules, and one draw needn't show every extreme that they name: `patch_col`: within each device's row the column numbers never fall, and each column holds 1 to 4 patch slots. `col_lu`: within each device's row the landunit numbers never fall, and each landunit holds 1 to 4 columns. `lu_grid`: within each device's row the gridcell numbers never fall, and each gridcell holds 1 to 4 landunits. `cell_target`: all devices' entries together are a permutation of 0 to 4095; the coupler owner of an entry q is q // 128, and each device's 128 gridcells go to 16 owners, exactly 8 to each.
All inputs are finite; a program needn't handle non-finite values.
Results may differ from a plain program's by a relative error of at most 0.0003.
Values sent between devices are 32-bit elements; how exact they have to be, the bound alone decides.
A program may use at most 64 MiB of HBM per device.

v0:
```python
import functools

import jax
import jax.numpy as jnp
from jax import lax
from jax.experimental import pallas as pl
from jax.experimental.pallas import tpu as pltpu
from jax.sharding import PartitionSpec as P

MESH = pl.DeviceIdType.MESH
F32 = jnp.float32
BF16 = jnp.bfloat16
INPUTS = 12


def iota(shape, dim):
    return lax.broadcasted_iota(jnp.int32, shape, dim)


def onehot(mask):
    return jnp.where(mask, 1.0, 0.0).astype(BF16)


def halves(x):
    high = x.astype(BF16)
    return high, (x - high.astype(F32)).astype(BF16)


def dot(a, b):
    return jnp.dot(a, b, preferred_element_type=F32)


def dot_nt(a, b):
    return lax.dot_general(a, b, (((1,), (1,)), ((), ())), preferred_element_type=F32)


def rows_of(rows, total):
    n = rows[0].shape[1]
    at = iota((total, n), 0)
    out = jnp.zeros((total, n), F32)
    for k, row in enumerate(rows):
        out = jnp.where(at == k, jnp.broadcast_to(row.astype(F32), (total, n)), out)
    return out.astype(BF16)


def split_by(x, size):
    if size & (size - 1) == 0:
        return lax.shift_right_logical(x, jnp.int32(size.bit_length() - 1)), x & (size - 1)
    return x // size, x % size


def select(table, chosen):
    high, low = halves(table)
    both = dot(jnp.concatenate([high, low], axis=0), chosen)
    return both[: table.shape[0]] + both[table.shape[0] :]


def pack(chosen, x):
    rows = chosen.shape[0] // 2
    pair = jnp.concatenate([chosen[:rows], chosen[rows:]], axis=1)
    blank = jnp.zeros(x.shape, BF16)

    def wide(part):
        upper = jnp.concatenate([part, blank], axis=1)
        return jnp.concatenate([upper, jnp.concatenate([blank, part], axis=1)], axis=0)

    high, low = halves(x)
    return dot_nt(pair, wide(high)) + dot_nt(pair, wide(low))


def unpack(packed):
    turned = packed.T
    middle = turned.shape[0] // 2
    return jnp.concatenate([turned[:middle], turned[middle:]], axis=1)


def kernel(
    n_clump, n_group, cap, half, stride,
    *refs,
):
    count_ref, *refs = refs
    sources, refs = refs[:INPUTS], refs[INPUTS:]
    merged_ref, anomaly_ref = refs[:2]
    send, recv, reply, back, ask, asked, send_sem, recv_sem, in_sem = refs[2:11]
    staged = refs[11:]
    loads = [
        pltpu.make_async_copy(source, into, in_sem.at[k])
        for k, (source, into) in enumerate(zip(sources, staged))
    ]
    (
        target_ref, lwt_ref, lgrid_ref, clu_ref, cwt_ref, pcol_ref, pwt_ref,
        scale_ref, pft_ref, flux_ref, frac_ref, field_ref,
    ) = staged
    n = n_clump * n_group
    my_clump, my_group = lax.axis_index("clump"), lax.axis_index("grp")

    def ahead_of(mine, step, size):
        there = mine + step
        return jnp.where(there >= size, there - size, there)

    def behind(mine, step, size):
        there = mine - step
        return jnp.where(there < 0, there + size, there)

    def each_other(act, there):
        groups = [there(my_group, g, n_group) for g in range(n_group)]

        def row(c, first):
            clump = there(my_clump, c, n_clump)
            for g in range(first, n_group):
                act(c * n_group + g, (clump, groups[g]))

        row(0, 1)
        if n_clump <= 8:
            for c in range(1, n_clump):
                row(c, 0)
        else:

            @pl.loop(1, n_clump)
            def _(c):
                row(c, 0)

    barrier = pltpu.get_barrier_semaphore()

    def greet(block, device):
        pl.semaphore_signal(barrier, inc=1, device_id=device, device_id_type=MESH)

    each_other(greet, ahead_of)
    for load in loads:
        load.start()

    nv, patches = flux_ref.shape
    types = scale_ref.shape[0]
    cols = cwt_ref.shape[1]
    lus = lwt_ref.shape[1]
    cells = target_ref.shape[1]
    rows = n * stride

    loads[0].wait()
    target = target_ref[...]
    owner, local = split_by(target, cells)
    owner_b = jnp.broadcast_to(owner.astype(F32), (cells, cells))
    same = owner_b == owner_b.T
    earlier = iota((cells, cells), 0) < iota((cells, cells), 1)
    rank = jnp.sum(jnp.where(same & earlier, 1.0, 0.0), axis=0, keepdims=True).astype(jnp.int32)
    to_clump, to_group = split_by(owner, n_group)
    block = behind(to_clump, my_clump, n_clump) * n_group
    block = (block + behind(to_group, my_group, n_group)) * stride
    from_block = behind(my_clump, to_clump, n_clump) * n_group
    from_block = (from_block + behind(my_group, to_group, n_group)) * stride
    part, line = split_by(rank, half)
    slot_of = onehot(iota((2 * rows, cells), 0) == part * rows + block + line)

    loads[10].wait()
    frac = frac_ref[...]
    at = iota((rows, cells), 0)
    asks = jnp.where(at == block, (local + 1).astype(F32), 0.0).astype(BF16)
    ask_rows = dot_nt(asks, onehot(iota((128, cells), 0) == rank))
    second = split_by(iota((rows, 128), 0), stride)[1] == 1
    ask[...] = jnp.where(second, jnp.broadcast_to(frac, (rows, cells)), ask_rows)
    asked[0:2, :] = ask[0:2, :]
    for load in loads[1:5]:
        load.wait()
    def copy(source, into, k, count, block, device):
        start = block * stride
        lines = pl.ds(start if isinstance(start, int) else pl.multiple_of(start, stride), count)
        return pltpu.make_async_remote_copy(
            src_ref=source.at[lines],
            dst_ref=into.at[lines],
            send_sem=send_sem.at[k],
            recv_sem=recv_sem.at[k],
            device_id=device,
            device_id_type=MESH,
        )

    def send_all(source, into, k, count, there):
        def one(block, device):
            copy(source, into, k, count, block, device).start()

        each_other(one, there)

    def wait(buffer, sem, count):
        rest = buffer.at[pl.ds(0, (n - 1) * count)]
        pltpu.make_async_copy(rest, rest, sem).wait()

    lu_hi, lu_lo = halves(lwt_ref[...])
    lu_rows = rows_of([lu_hi, lu_lo, lgrid_ref[...]], 16)
    lu_of = onehot(iota((lus, cols), 0) == clu_ref[...])
    col_vals = dot(lu_rows, lu_of)
    col_w = cwt_ref[...] * (col_vals[0:1] + col_vals[1:2])
    pl.semaphore_wait(barrier, n - 1)
    send_all(ask, asked, 0, 2, ahead_of)

    for load in loads[5:7]:
        load.wait()
    c_hi, c_lo = halves(col_w)
    col_rows = rows_of([c_hi, c_lo, col_vals[2:3]], 16)
    col_of = onehot(iota((cols, patches), 0) == pcol_ref[...])
    patch_vals = dot(col_rows, col_of)
    alive = jnp.where(iota((1, patches), 1) < count_ref[0], 1.0, 0.0)
    weight = alive * pwt_ref[...] * (patch_vals[0:1] + patch_vals[1:2])
    home = patch_vals[2:3].astype(jnp.int32)
    home_of = onehot(iota((cells, patches), 0) == home)

    for load in loads[7:10]:
        load.wait()
    table = scale_ref[...]
    t1 = table.astype(BF16).astype(F32)
    t2 = (table - t1).astype(BF16).astype(F32)
    t3 = table - t1 - t2
    pad = 128 - 3 * types
    stacked = jnp.concatenate([t1, t2, t3, jnp.zeros((pad, nv), F32)], axis=0)
    stacked = jnp.concatenate([stacked, jnp.zeros((128, 128 - nv), F32)], axis=1)
    scale_t = stacked.T[:nv].astype(BF16)
    kind = iota((128, patches), 0)
    type_of = onehot(
        (kind == pft_ref[...])
        | (kind == pft_ref[...] + types)
        | (kind == pft_ref[...] + 2 * types)
    )
    scaled = flux_ref[...] * dot(scale_t, type_of)

    x_hi, x_lo = halves(scaled * weight)
    w_hi, w_lo = halves(weight)
    sums = dot_nt(
        jnp.concatenate([x_hi, x_lo, rows_of([w_hi, w_lo], 16)], axis=0), home_of
    )
    num = sums[:nv] + sums[nv : 2 * nv]
    den = sums[2 * nv : 2 * nv + 1] + sums[2 * nv + 1 : 2 * nv + 2]
    mean = num / jnp.maximum(den, 1.0)

    send[...] = pack(slot_of, mean)
    recv[0:half, :] = send[0:half, :]
    send_all(send, recv, 1, half, ahead_of)

    loads[11].wait()
    other = (1.0 - frac) * field_ref[...]
    lane = iota((2 * rows, 128), 0)
    lane_part = jnp.where(lane >= rows, 1, 0)
    lane_line = split_by(lane - lane_part * rows, stride)[1]
    its_lane = (lane_line < half) & (
        iota((2 * rows, 128), 1) == lane_part * half + lane_line
    )
    in_two = split_by(iota((rows, 128), 0), stride)[1] < 2
    in_half = split_by(iota((rows, 128), 0), stride)[1] < half
    wait(asked, recv_sem.at[0], 2)
    told = jnp.where(in_two, asked[...], 0.0)
    ids_of = jnp.broadcast_to(
        told.reshape(n, stride, 128)[:, 0:1, :], (n, stride, 128)
    ).reshape(rows, 128)
    spread = jnp.where(its_lane, jnp.concatenate([ids_of, ids_of], axis=0), 0.0).astype(BF16)
    ids = dot(spread, jnp.ones((128, cells), BF16))
    owned_of = onehot(ids == (iota((2 * rows, cells), 1) + 1).astype(F32))
    reply[...] = pack(owned_of, other)
    back[0:half, :] = reply[0:half, :]
    send_all(reply, back, 2, half, behind)

    all_frac = select(told.T, onehot(iota((rows, cells), 0) == from_block + 1))
    cell_frac = jnp.sum(
        jnp.where(iota((128, cells), 0) == local, all_frac, 0.0), axis=0, keepdims=True
    )
    land_part = cell_frac * mean

    wait(recv, recv_sem.at[1], half)
    owned = select(unpack(jnp.where(in_half, recv[...], 0.0)), owned_of)
    merged_ref[...] = frac * owned + other

    wait(back, recv_sem.at[2], half)
    cell = land_part + select(unpack(jnp.where(in_half, back[...], 0.0)), slot_of)
    anomaly_ref[...] = alive * (scaled - select(cell, home_of))
    wait(ask, send_sem.at[0], 2)
    wait(send, send_sem.at[1], half)
    wait(reply, send_sem.at[2], half)


def store_kernel(merged, anomaly, merged_out, anomaly_out, sem):
    stores = [
        pltpu.make_async_copy(merged, merged_out, sem.at[0]),
        pltpu.make_async_copy(anomaly, anomaly_out, sem.at[1]),
    ]
    for store in stores:
        store.start()
    for store in stores:
        store.wait()


def per_device(
    flux, patch_pft, patch_wt, patch_col, col_wt, col_lu, lu_wt, lu_grid, cell_target,
    patch_count, pft_scale, cpl_frac, cpl_field,
):
    n_clump = lax.axis_size("clump")
    n_group = lax.axis_size("grp")
    n = n_clump * n_group
    nv = flux.shape[2]
    patches = flux.shape[1]
    cells = cell_target.shape[1]
    cap = max(2, 2 * cells // n)
    half = -(-cap // 2)
    stride = -(-max(half, 2) // 8) * 8
    vmem = pl.BlockSpec(memory_space=pltpu.VMEM)
    hbm = pl.BlockSpec(memory_space=pltpu.HBM)
    buffer = pltpu.VMEM((n * stride, 128), F32)
    inputs = (
        cell_target, lu_wt, lu_grid, col_lu, col_wt, patch_col, patch_wt,
        pft_scale, patch_pft, flux[0].T, cpl_frac.reshape(1, -1), cpl_field.T,
    )
    shapes = (
        jax.ShapeDtypeStruct((nv, cells), F32),
        jax.ShapeDtypeStruct((nv, patches), F32),
    )
    results = pl.pallas_call(
        functools.partial(kernel, n_clump, n_group, cap, half, stride),
        out_shape=tuple(pltpu.VMEM(x.shape, x.dtype) for x in shapes),
        in_specs=[pl.BlockSpec(memory_space=pltpu.SMEM)] + [hbm] * INPUTS,
        out_specs=(vmem, vmem),
        scratch_shapes=[
            buffer, buffer, buffer, buffer, buffer, buffer,
            pltpu.SemaphoreType.DMA((3,)),
            pltpu.SemaphoreType.DMA((3,)),
            pltpu.SemaphoreType.DMA((INPUTS,)),
        ]
        + [
            pltpu.VMEM(x.shape, x.dtype)
            for x in inputs
        ],
        compiler_params=pltpu.CompilerParams(
            collective_id=0, has_side_effects=True, vmem_limit_bytes=48 * 1024 * 1024
        ),
    )(patch_count, *[pltpu.with_memory_space_constraint(x, pltpu.HBM) for x in inputs])
    merged, anomaly = pl.pallas_call(
        store_kernel,
        out_shape=shapes,
        in_specs=[vmem, vmem],
        out_specs=(hbm, hbm),
        scratch_shapes=[pltpu.SemaphoreType.DMA((2,))],
        compiler_params=pltpu.CompilerParams(vmem_limit_bytes=4 * 1024 * 1024),
    )(*results)
    return merged.T, anomaly.T[None]


def solution(mesh):
    split = P(("clump", "grp"))
    return jax.shard_map(
        per_device,
        mesh=mesh,
        in_specs=(split,) * 10 + (P(),) + (split,) * 2,
        out_specs=(split, split),
        check_vma=False,
    )
```

profile of v0, /device:TPU:0, one launch (start us, length us, event | category | flops | bytes accessed | tf_op | source)
XLA Modules:
  0.0 19.5 jit_solution(18323764847359225401)
XLA Ops:
  1.3 17.5 %shard_map.140 = (f32[64,128]{1,0:T(8,128)S(1)}, f32[64,1024]{1,0:T(8,128)S(1)}) custom-call(s32[1]{0:T(128)S(6)} %copy.15.refs_0_, s32[1,128]{1,0:T(1,128)} %refs_1_.1, f32[1,256]{1,0:T(1,128)} %refs_2_.1, s32[1,256]{1,0:T(1,128)} %refs_3_.1, s32[1,512]{1,0:T(1,128)} %refs_4_.1, f32[1,512]{1,0:T(1,128)} %refs_5_.1, s32[1,1024]{1,0:T(1,128)} %refs_6_.1, ...), custom_call_target="tpu_custom_call" | custom-call | tf_op jit(solution)/shard_map/pallas_call | solution.py:311
  18.8 0.7 %shard_map.141 = (f32[64,128]{1,0:T(8,128)}, f32[64,1024]{1,0:T(8,128)}) custom-call(f32[64,128]{1,0:T(8,128)S(1)} %get-tuple-element.6.merged, f32[64,1024]{1,0:T(8,128)S(1)} %get-tuple-element.7.anomaly), custom_call_target="tpu_custom_call" | custom-call | tf_op jit(solution)/shard_map/pallas_call | solution.py:330
where the time goes:
time: 19.7 us; the launch traced here: 19.5 us
  Pallas kernels  18.2 us (92%)
  between operations  1.29 us (7%)
    pallas_call x1, Pallas kernels, per_device(): pl.pallas_call(functools.partial(kernel, n_clump, n_group, cap, half, str...  17.5 us
    pallas_call x1, Pallas kernels, per_device(): pl.pallas_call(store_kernel, out_shape=shapes, in_specs=[vmem, vmem], out...  0.73 us

commit v1 on v0

v1 whole, which is shorter than its diff:
```python
import functools

import jax
import jax.numpy as jnp
from jax import lax
from jax.experimental import pallas as pl
from jax.experimental.pallas import tpu as pltpu
from jax.sharding import PartitionSpec as P

MESH = pl.DeviceIdType.MESH
F32 = jnp.float32
BF16 = jnp.bfloat16
INPUTS = 12


def iota(shape, dim):
    return lax.broadcasted_iota(jnp.int32, shape, dim)


def onehot(mask):
    return jnp.where(mask, 1.0, 0.0).astype(BF16)


def halves(x):
    high = x.astype(BF16)
    return high, (x - high.astype(F32)).astype(BF16)


def dot(a, b):
    return jnp.dot(a, b, preferred_element_type=F32)


def dot_nt(a, b):
    return lax.dot_general(a, b, (((1,), (1,)), ((), ())), preferred_element_type=F32)


def rows_of(rows, total):
    n = rows[0].shape[1]
    at = iota((total, n), 0)
    out = jnp.zeros((total, n), F32)
    for k, row in enumerate(rows):
        out = jnp.where(at == k, jnp.broadcast_to(row.astype(F32), (total, n)), out)
    return out.astype(BF16)


def split_by(x, size):
    if size & (size - 1) == 0:
        return lax.shift_right_logical(x, jnp.int32(size.bit_length() - 1)), x & (size - 1)
    return x // size, x % size


def select(table, chosen):
    high, low = halves(table)
    both = dot(jnp.concatenate([high, low], axis=0), chosen)
    return both[: table.shape[0]] + both[table.shape[0] :]


def pack_two(chosen, one, two):
    rows = chosen.shape[0] // 2
    pair = jnp.concatenate([chosen[:rows], chosen[rows:]], axis=1)
    blank = jnp.zeros(one.shape, BF16)

    def wide(first, second):
        upper = jnp.concatenate([first, blank], axis=1)
        return jnp.concatenate([upper, jnp.concatenate([blank, second], axis=1)], axis=0)

    (high, low), (high_two, low_two) = halves(one), halves(two)
    return dot_nt(pair, wide(high, high_two)) + dot_nt(pair, wide(low, low_two))


def pack(chosen, x):
    return pack_two(chosen, x, x)


def unpack(packed):
    turned = packed.T
    middle = turned.shape[0] // 2
    return jnp.concatenate([turned[:middle], turned[middle:]], axis=1)


def kernel(
    n_clump, n_group, inner_clump, inner_group, cap, slots, half, stride,
    *refs,
):
    count_ref, *refs = refs
    sources, refs = refs[:INPUTS], refs[INPUTS:]
    merged_ref, anomaly_ref = refs[:2]
    tables, ask, asked, reply, back, send, recv = refs[2:9]
    send_sem, recv_sem, in_sem, ready = refs[9:13]
    staged = refs[13:]
    (
        target_ref, lwt_ref, lgrid_ref, clu_ref, cwt_ref, pcol_ref, pwt_ref,
        scale_ref, pft_ref, flux_ref,
    ) = staged
    nv, patches = flux_ref.shape
    types = scale_ref.shape[0]
    cols = cwt_ref.shape[1]
    lus = lwt_ref.shape[1]
    cells = target_ref.shape[1]
    n = n_clump * n_group
    rows = n * stride
    outer_clump, outer_group = n_clump // inner_clump, n_group // inner_group
    sharers, askers = inner_clump * outer_group, outer_clump * inner_group
    pairs = sharers // 2
    field_ref, frac_ref = tables.at[0, pl.ds(0, nv)], tables.at[0, pl.ds(nv, 1)]
    loads = [
        pltpu.make_async_copy(source, into, in_sem.at[k])
        for k, (source, into) in enumerate(zip(sources, (*staged, frac_ref, field_ref)))
    ]
    my_clump, my_group = lax.axis_index("clump"), lax.axis_index("grp")
    my_slab, my_row = lax.div(my_clump, inner_clump), lax.rem(my_clump, inner_clump)
    my_side, my_core = lax.div(my_group, inner_group), lax.rem(my_group, inner_group)

    def ahead_of(mine, step, size):
        there = mine + step
        return jnp.where(there >= size, there - size, there)

    def behind(mine, step, size):
        there = mine - step
        return jnp.where(there < 0, there + size, there)

    def others(act, outer, inner):
        for i in range(1, inner):
            act(i, 0, i)
        if outer <= 8:
            for o in range(1, outer):
                for i in range(inner):
                    act(o * inner + i, o, i)
        else:

            @pl.loop(1, outer)
            def _(o):
                for i in range(inner):
                    act(o * inner + i, o, i)

    def each_sharer(act, there):
        def one(block, o, i):
            row, side = there(my_row, o, inner_clump), there(my_side, i, outer_group)
            act(block, (my_slab * inner_clump + row, side * inner_group + my_core))

        others(one, inner_clump, outer_group)

    def each_asker(act, there):
        def one(block, o, i):
            slab, core = there(my_slab, o, outer_clump), there(my_core, i, inner_group)
            act(block, (slab * inner_clump + my_row, my_side * inner_group + core))

        others(one, outer_clump, inner_group)

    def each_other(act, there):
        def one(block, o, i):
            act(block, (there(my_clump, o, n_clump), there(my_group, i, n_group)))

        others(one, n_clump, n_group)

    def remote(source, into, k, device):
        pltpu.make_async_remote_copy(
            src_ref=source,
            dst_ref=into,
            send_sem=send_sem.at[k],
            recv_sem=recv_sem.at[k],
            device_id=device,
            device_id_type=MESH,
        ).start()

    def wait(rest, sem):
        pltpu.make_async_copy(rest, rest, sem).wait()

    barrier = pltpu.get_barrier_semaphore()

    def greet(block, device):
        pl.semaphore_signal(barrier, inc=1, device_id=device, device_id_type=MESH)

    each_asker(greet, ahead_of)
    each_sharer(greet, ahead_of)
    for k in (11, 10, *range(10)):
        loads[k].start()

    table_rows = pl.ds(0, nv + 1)
    loads[10].wait()
    loads[11].wait()
    pl.semaphore_wait(barrier, sharers + askers - 2)

    def share(block, device):
        remote(tables.at[0, table_rows], tables.at[block, table_rows], 0, device)

    each_sharer(share, ahead_of)

    def tell(block, device):
        pl.semaphore_signal(ready, inc=1, device_id=device, device_id_type=MESH)

    each_sharer(tell, ahead_of)

    loads[0].wait()
    target = target_ref[...]
    owner, local = split_by(target, cells)
    owner_b = jnp.broadcast_to(owner.astype(F32), (cells, cells))
    same = owner_b == owner_b.T
    earlier = iota((cells, cells), 0) < iota((cells, cells), 1)
    rank = jnp.sum(jnp.where(same & earlier, 1.0, 0.0), axis=0, keepdims=True).astype(jnp.int32)
    to_clump, to_group = split_by(owner, n_group)
    to_slab, to_row = split_by(to_clump, inner_clump)
    to_side, to_core = split_by(to_group, inner_group)
    table = behind(my_row, to_row, inner_clump) * outer_group
    table = table + behind(my_side, to_side, outer_group)
    holder = behind(to_slab, my_slab, outer_clump) * inner_group
    holder = holder + behind(to_core, my_core, inner_group)
    wanted = (local + 1).astype(F32)
    asks = jnp.where(iota((askers, cells), 0) == holder, wanted, 0.0).astype(BF16)
    ask_rows = dot_nt(asks, onehot(iota((128, cells), 0) == table * slots + rank))
    for k in range(askers):
        ask[k, 0:1, :] = ask_rows[k : k + 1]
    asked[0, 0:1, :] = ask_rows[0:1]
    one_row = pl.ds(0, 1)

    def request(block, device):
        remote(ask.at[block, one_row], asked.at[block, one_row], 1, device)

    each_asker(request, ahead_of)

    frac = frac_ref[...]
    block = behind(to_clump, my_clump, n_clump) * n_group
    block = (block + behind(to_group, my_group, n_group)) * stride
    from_block = behind(my_clump, to_clump, n_clump) * n_group
    from_block = (from_block + behind(my_group, to_group, n_group)) * stride
    part, line = split_by(rank, half)
    slot_of = onehot(iota((2 * rows, cells), 0) == part * rows + block + line)
    at = iota((rows, cells), 0)
    asks = jnp.where(at == block + half, wanted, 0.0).astype(BF16)
    id_rows = dot_nt(asks, onehot(iota((128, cells), 0) == rank))
    in_stride = split_by(iota((rows, 128), 0), stride)[1]
    extra = jnp.where(in_stride == half + 1, jnp.broadcast_to(frac, (rows, cells)), id_rows)

    for load in loads[1:5]:
        load.wait()
    lu_hi, lu_lo = halves(lwt_ref[...])
    lu_rows = rows_of([lu_hi, lu_lo, lgrid_ref[...]], 16)
    lu_of = onehot(iota((lus, cols), 0) == clu_ref[...])
    col_vals = dot(lu_rows, lu_of)
    col_w = cwt_ref[...] * (col_vals[0:1] + col_vals[1:2])

    for load in loads[5:7]:
        load.wait()
    c_hi, c_lo = halves(col_w)
    col_rows = rows_of([c_hi, c_lo, col_vals[2:3]], 16)
    col_of = onehot(iota((cols, patches), 0) == pcol_ref[...])
    patch_vals = dot(col_rows, col_of)
    alive = jnp.where(iota((1, patches), 1) < count_ref[0], 1.0, 0.0)
    weight = alive * pwt_ref[...] * (patch_vals[0:1] + patch_vals[1:2])
    home = patch_vals[2:3].astype(jnp.int32)
    home_of = onehot(iota((cells, patches), 0) == home)

    for load in loads[7:10]:
        load.wait()
    scales = scale_ref[...]
    t1 = scales.astype(BF16).astype(F32)
    t2 = (scales - t1).astype(BF16).astype(F32)
    t3 = scales - t1 - t2
    pad = 128 - 3 * types
    stacked = jnp.concatenate([t1, t2, t3, jnp.zeros((pad, nv), F32)], axis=0)
    stacked = jnp.concatenate([stacked, jnp.zeros((128, 128 - nv), F32)], axis=1)
    scale_t = stacked.T[:nv].astype(BF16)
    kind = iota((128, patches), 0)
    type_of = onehot(
        (kind == pft_ref[...])
        | (kind == pft_ref[...] + types)
        | (kind == pft_ref[...] + 2 * types)
    )
    scaled = flux_ref[...] * dot(scale_t, type_of)

    x_hi, x_lo = halves(scaled * weight)
    w_hi, w_lo = halves(weight)
    sums = dot_nt(
        jnp.concatenate([x_hi, x_lo, rows_of([w_hi, w_lo], 16)], axis=0), home_of
    )
    num = sums[:nv] + sums[nv : 2 * nv]
    den = sums[2 * nv : 2 * nv + 1] + sums[2 * nv + 1 : 2 * nv + 2]
    mean = num / jnp.maximum(den, 1.0)

    send[...] = jnp.where(in_stride < half, pack(slot_of, mean), extra)
    lines = half + 2
    recv[0:lines, :] = send[0:lines, :]
    pl.semaphore_wait(ready, sharers - 1)

    def give(block, device):
        start = block * stride
        start = start if isinstance(start, int) else pl.multiple_of(start, stride)
        its = pl.ds(start, lines)
        remote(send.at[its], recv.at[its], 2, device)

    each_other(give, ahead_of)

    wait(asked.at[pl.ds(1, askers - 1), one_row], recv_sem.at[1])
    told = jnp.broadcast_to(asked[...][:, 0:1, :], (askers, slots, 128)).reshape(askers * slots, 128)
    lane_less = iota((askers * slots, 128), 1) - split_by(iota((askers * slots, 128), 0), slots)[1]
    spread = [jnp.where(lane_less == t * slots, told, 0.0) for t in range(sharers)]
    ids = dot(jnp.concatenate(spread, axis=0).astype(BF16), jnp.ones((128, cells), BF16))
    held_of = onehot(ids == (iota(ids.shape, 1) + 1).astype(F32))

    wait(tables.at[pl.ds(1, sharers - 1), table_rows], recv_sem.at[0])
    for p in range(pairs):
        one, two = 2 * p * askers * slots, (2 * p + 1) * askers * slots
        chosen = held_of[one : two + askers * slots]
        both = [(1.0 - tables[t, nv : nv + 1]) * tables[t, 0:nv] for t in (2 * p, 2 * p + 1)]
        reply[:, p * slots : (p + 1) * slots, :] = pack_two(chosen, *both).reshape(askers, slots, 128)
    back[0] = reply[0]

    def respond(block, device):
        remote(reply.at[block], back.at[block], 3, device)

    each_asker(respond, behind)

    other = (1.0 - frac) * field_ref[...]
    lane = iota((2 * rows, 128), 0)
    lane_part = jnp.where(lane >= rows, 1, 0)
    lane_line = split_by(lane - lane_part * rows, stride)[1]
    its_lane = (lane_line < half) & (
        iota((2 * rows, 128), 1) == lane_part * half + lane_line
    )
    pair, side = split_by(table, 2)
    place = side * (askers * pairs * slots) + (holder * pairs + pair) * slots + rank
    answer_of = onehot(iota((2 * askers * pairs * slots, cells), 0) == place)

    flat = [pl.ds(0, (n - 1) * lines), pl.ds(0, n * stride)]
    wait(recv.at[flat[0]], recv_sem.at[2])
    got = jnp.where(in_stride < lines, recv[...], 0.0)
    by_device = got.reshape(n, stride, 128)
    ids_of = jnp.broadcast_to(by_device[:, half : half + 1, :], (n, stride, 128)).reshape(rows, 128)
    spread = jnp.where(its_lane, jnp.concatenate([ids_of, ids_of], axis=0), 0.0).astype(BF16)
    ids = dot(spread, jnp.ones((128, cells), BF16))
    owned_of = onehot(ids == (iota((2 * rows, cells), 1) + 1).astype(F32))
    owned = select(unpack(jnp.where(in_stride < half, got, 0.0)), owned_of)
    merged_ref[...] = frac * owned + other

    all_frac = select(got.T, onehot(at == from_block + half + 1))
    cell_frac = jnp.sum(
        jnp.where(iota((128, cells), 0) == local, all_frac, 0.0), axis=0, keepdims=True
    )
    land_part = cell_frac * mean

    wait(back.at[pl.ds(1, askers - 1)], recv_sem.at[3])
    answers = back[...].reshape(askers * pairs * slots, 128)
    cell = land_part + select(unpack(answers), answer_of)
    anomaly_ref[...] = alive * (scaled - select(cell, home_of))
    wait(tables.at[pl.ds(1, sharers - 1), table_rows], send_sem.at[0])
    wait(ask.at[pl.ds(1, askers - 1), one_row], send_sem.at[1])
    wait(send.at[flat[0]], send_sem.at[2])
    wait(reply.at[pl.ds(1, askers - 1)], send_sem.at[3])


def store_kernel(merged, anomaly, merged_out, anomaly_out, sem):
    stores = [
        pltpu.make_async_copy(merged, merged_out, sem.at[0]),
        pltpu.make_async_copy(anomaly, anomaly_out, sem.at[1]),
    ]
    for store in stores:
        store.start()
    for store in stores:
        store.wait()


def per_device(
    flux, patch_pft, patch_wt, patch_col, col_wt, col_lu, lu_wt, lu_grid, cell_target,
    patch_count, pft_scale, cpl_frac, cpl_field,
):
    n_clump = lax.axis_size("clump")
    n_group = lax.axis_size("grp")
    n = n_clump * n_group
    nv = flux.shape[2]
    patches = flux.shape[1]
    cells = cell_target.shape[1]
    inner_group = 2 if n_group % 2 == 0 else 1
    outer_group = n_group // inner_group
    inner_clump = outer_group if n_clump % outer_group == 0 else 1
    sharers = inner_clump * outer_group
    askers = n // sharers
    cap = max(2, 2 * cells // n)
    half = -(-cap // 2)
    slots = -(-cap // 8) * 8
    stride = -(-(half + 2) // 8) * 8
    vmem = pl.BlockSpec(memory_space=pltpu.VMEM)
    hbm = pl.BlockSpec(memory_space=pltpu.HBM)
    staged = (
        cell_target, lu_wt, lu_grid, col_lu, col_wt, patch_col, patch_wt,
        pft_scale, patch_pft, flux[0].T,
    )
    inputs = (*staged, cpl_frac.reshape(1, -1), cpl_field.T)
    shapes = (
        jax.ShapeDtypeStruct((nv, cells), F32),
        jax.ShapeDtypeStruct((nv, patches), F32),
    )
    results = pl.pallas_call(
        functools.partial(
            kernel, n_clump, n_group, inner_clump, inner_group, cap, slots, half, stride
        ),
        out_shape=tuple(pltpu.VMEM(x.shape, x.dtype) for x in shapes),
        in_specs=[pl.BlockSpec(memory_space=pltpu.SMEM)] + [hbm] * INPUTS,
        out_specs=(vmem, vmem),
        scratch_shapes=[
            pltpu.VMEM((sharers, -(-(nv + 1) // 8) * 8, cells), F32),
            pltpu.VMEM((askers, 8, 128), F32),
            pltpu.VMEM((askers, 8, 128), F32),
            pltpu.VMEM((askers, sharers // 2 * slots, 128), F32),
            pltpu.VMEM((askers, sharers // 2 * slots, 128), F32),
            pltpu.VMEM((n * stride, 128), F32),
            pltpu.VMEM((n * stride, 128), F32),
            pltpu.SemaphoreType.DMA((4,)),
            pltpu.SemaphoreType.DMA((4,)),
            pltpu.SemaphoreType.DMA((INPUTS,)),
            pltpu.SemaphoreType.REGULAR,
        ]
        + [pltpu.VMEM(x.shape, x.dtype) for x in staged],
        compiler_params=pltpu.CompilerParams(
            collective_id=0, has_side_effects=True, vmem_limit_bytes=48 * 1024 * 1024
        ),
    )(patch_count, *[pltpu.with_memory_space_constraint(x, pltpu.HBM) for x in inputs])
    merged, anomaly = pl.pallas_call(
        store_kernel,
        out_shape=shapes,
        in_specs=[vmem, vmem],
        out_specs=(hbm, hbm),
        scratch_shapes=[pltpu.SemaphoreType.DMA((2,))],
        compiler_params=pltpu.CompilerParams(vmem_limit_bytes=4 * 1024 * 1024),
    )(*results)
    return merged.T, anomaly.T[None]


def solution(mesh):
    split = P(("clump", "grp"))
    return jax.shard_map(
        per_device,
        mesh=mesh,
        in_specs=(split,) * 10 + (P(),) + (split,) * 2,
        out_specs=(split, split),
        check_vma=False,
    )
```

time: 19.7 us -> 16 us (0.81)
  Pallas kernels: 18.2 us -> 14.5 us
    pallas_call x1, Pallas kernels: 17.5 us -> 13.8 us  [per_device(): pl.pallas_call(functools.partial(kernel, n_clump, n_group, inner_clump, i...]
where the time goes in v1:
time: 16 us; the launch traced here: 15.8 us
  Pallas kernels  14.5 us (91%)
  between operations  1.29 us (8%)
    pallas_call x1, Pallas kernels, per_device(): pl.pallas_call(functools.partial(kernel, n_clump, n_group, inner_clump, i...  13.8 us
    pallas_call x1, Pallas kernels, per_device(): pl.pallas_call(store_kernel, out_shape=shapes, in_specs=[vmem, vmem], out...  0.73 us

profile of v1, /device:TPU:0, one launch (start us, length us, event | category | flops | bytes accessed | tf_op | source)
XLA Modules:
  0.0 15.8 jit_solution(11097440368225894867)
XLA Ops:
  1.3 13.8 %shard_map.140 = (f32[64,128]{1,0:T(8,128)S(1)}, f32[64,1024]{1,0:T(8,128)S(1)}) custom-call(s32[1]{0:T(128)S(6)} %copy.15.refs_0_, s32[1,128]{1,0:T(1,128)} %refs_1_.1, f32[1,256]{1,0:T(1,128)} %refs_2_.1, s32[1,256]{1,0:T(1,128)} %refs_3_.1, s32[1,512]{1,0:T(1,128)} %refs_4_.1, f32[1,512]{1,0:T(1,128)} %refs_5_.1, s32[1,1024]{1,0:T(1,128)} %refs_6_.1, ...), custom_call_target="tpu_custom_call" | custom-call | tf_op jit(solution)/shard_map/pallas_call | solution.py:392
  15.1 0.7 %shard_map.141 = (f32[64,128]{1,0:T(8,128)}, f32[64,1024]{1,0:T(8,128)}) custom-call(f32[64,128]{1,0:T(8,128)S(1)} %get-tuple-element.6.merged, f32[64,1024]{1,0:T(8,128)S(1)} %get-tuple-element.7.anomaly), custom_call_target="tpu_custom_call" | custom-call | tf_op jit(solution)/shard_map/pallas_call | solution.py:417

commit v2 on v1

v2 whole, which is shorter than its diff:
```python
import functools

import jax
import jax.numpy as jnp
from jax import lax
from jax.experimental import pallas as pl
from jax.experimental.pallas import tpu as pltpu
from jax.sharding import PartitionSpec as P

MESH = pl.DeviceIdType.MESH
F32 = jnp.float32
BF16 = jnp.bfloat16
INPUTS = 12


def iota(shape, dim):
    return lax.broadcasted_iota(jnp.int32, shape, dim)


def onehot(mask):
    return jnp.where(mask, 1.0, 0.0).astype(BF16)


def halves(x):
    high = x.astype(BF16)
    return high, (x - high.astype(F32)).astype(BF16)


def dot(a, b):
    return jnp.dot(a, b, preferred_element_type=F32)


def dot_nt(a, b):
    return lax.dot_general(a, b, (((1,), (1,)), ((), ())), preferred_element_type=F32)


def rows_of(rows, total):
    n = rows[0].shape[1]
    at = iota((total, n), 0)
    out = jnp.zeros((total, n), F32)
    for k, row in enumerate(rows):
        out = jnp.where(at == k, jnp.broadcast_to(row.astype(F32), (total, n)), out)
    return out.astype(BF16)


def split_by(x, size):
    if size & (size - 1) == 0:
        return lax.shift_right_logical(x, jnp.int32(size.bit_length() - 1)), x & (size - 1)
    return x // size, x % size


def select(table, chosen):
    high, low = halves(table)
    both = dot(jnp.concatenate([high, low], axis=0), chosen)
    return both[: table.shape[0]] + both[table.shape[0] :]


def wide(one, two):
    blank = jnp.zeros(one.shape, BF16)

    def beside(first, second):
        upper = jnp.concatenate([first, blank], axis=1)
        return jnp.concatenate([upper, jnp.concatenate([blank, second], axis=1)], axis=0)

    (high, low), (high_two, low_two) = halves(one), halves(two)
    return beside(high, high_two), beside(low, low_two)


def pack_wide(chosen, parts):
    rows = chosen.shape[0] // 2
    pair = jnp.concatenate([chosen[:rows], chosen[rows:]], axis=1)
    return dot_nt(pair, parts[0]) + dot_nt(pair, parts[1])


def pack(chosen, x):
    return pack_wide(chosen, wide(x, x))


def unpack(packed):
    turned = packed.T
    middle = turned.shape[0] // 2
    return jnp.concatenate([turned[:middle], turned[middle:]], axis=1)


def kernel(
    n_clump, n_group, inner_clump, inner_group, cap, slots, half, stride,
    *refs,
):
    count_ref, *refs = refs
    sources, refs = refs[:INPUTS], refs[INPUTS:]
    merged_ref, anomaly_ref = refs[:2]
    tables, own, ask, asked, note, noted, reply, back, send, recv = refs[2:12]
    send_sem, recv_sem, in_sem, known, column = refs[12:17]
    staged = refs[17:]
    (
        target_ref, lwt_ref, lgrid_ref, clu_ref, cwt_ref, pcol_ref, pwt_ref,
        scale_ref, pft_ref, flux_ref,
    ) = staged
    nv, patches = flux_ref.shape
    types = scale_ref.shape[0]
    cols = cwt_ref.shape[1]
    lus = lwt_ref.shape[1]
    cells = target_ref.shape[1]
    n = n_clump * n_group
    rows = n * stride
    outer_clump, outer_group = n_clump // inner_clump, n_group // inner_group
    places, askers = inner_clump * outer_group, outer_clump * inner_group
    sharers = places * inner_group
    pairs = sharers // 2
    field_ref, frac_ref = own.at[pl.ds(0, nv)], own.at[pl.ds(nv, 1)]
    loads = [
        pltpu.make_async_copy(source, into, in_sem.at[k])
        for k, (source, into) in enumerate(zip(sources, (*staged, frac_ref, field_ref)))
    ]
    my_clump, my_group = lax.axis_index("clump"), lax.axis_index("grp")
    my_slab, my_row = lax.div(my_clump, inner_clump), lax.rem(my_clump, inner_clump)
    my_side, my_core = lax.div(my_group, inner_group), lax.rem(my_group, inner_group)
    keeper = inner_group - 1
    keeps = my_core == keeper

    def ahead_of(mine, step, size):
        there = mine + step
        return jnp.where(there >= size, there - size, there)

    def behind(mine, step, size):
        there = mine - step
        return jnp.where(there < 0, there + size, there)

    def offsets(act, outer, inner, own=False, far_first=False):
        if outer <= 8:
            steps = [(o, i) for o in range(outer) for i in range(inner) if own or o or i]
            for o, i in steps[::-1] if far_first else steps:
                act(o * inner + i, o, i)
        else:
            for i in range(0 if own else 1, inner):
                act(i, 0, i)

            @pl.loop(1, outer)
            def _(o):
                for i in range(inner):
                    act(o * inner + i, o, i)

    def place(there, row, side, slab, core):
        slab, row = there(my_slab, slab, outer_clump), there(my_row, row, inner_clump)
        side, core = there(my_side, side, outer_group), there(my_core, core, inner_group)
        return slab * inner_clump + row, side * inner_group + core

    def each_other(act, there):
        for row in range(inner_clump - 1, -1, -1):
            for side in range(outer_group - 1, -1, -1):
                t = row * outer_group + side

                def one(block, o, i, t=t, row=row, side=side):
                    act(t * askers + block, place(there, row, side, o, i))

                offsets(one, outer_clump, inner_group, own=t > 0)

    def remote(source, into, k, device):
        pltpu.make_async_remote_copy(
            src_ref=source,
            dst_ref=into,
            send_sem=send_sem.at[k],
            recv_sem=recv_sem.at[k],
            device_id=device,
            device_id_type=MESH,
        ).start()

    def wait(rest, sem):
        pltpu.make_async_copy(rest, rest, sem).wait()

    barrier = pltpu.get_barrier_semaphore()

    def signal(sem, device):
        pl.semaphore_signal(sem, inc=1, device_id=device, device_id_type=MESH)

    def when_places(act, there, first, second):
        def one(block, o, i):
            @pl.when((first + o < inner_clump) & (second + i < outer_group))
            def _():
                act(block, place(there, o, i, 0, 0))

        offsets(one, inner_clump, outer_group)

    def slabs(act):
        if outer_clump <= 8:
            for o in range(1, outer_clump):
                act(o)
        else:
            pl.loop(1, outer_clump)(act)

    def when_slabs(act, there, first):
        def one(o):
            @pl.when(first + o < outer_clump)
            def _():
                act(o, place(there, 0, 0, o, 0))

        slabs(one)

    def keeper_of(device):
        return device[0], device[1] - my_core + keeper

    def greet(block, device):
        signal(barrier, keeper_of(device))

        @pl.when(keeps)
        def _():
            for core in range(keeper):
                signal(barrier, (device[0], device[1] - my_core + core))

    up_row, up_side = inner_clump - 1 - my_row, outer_group - 1 - my_side
    up_slab = outer_clump - 1 - my_slab
    last_place, last_plane = up_row + up_side == 0, up_slab == 0
    last = last_place & last_plane & keeps
    when_slabs(greet, ahead_of, my_slab)
    when_places(greet, ahead_of, my_row, my_side)
    mates = [(my_clump, my_group - my_core + core) for core in range(inner_group)]

    @pl.when(keeps)
    def _():
        for core in range(keeper):
            signal(barrier, mates[core])

    @pl.when((last_place == last_plane) & jnp.logical_not(last))
    def _():
        signal(barrier, (n_clump - 1, n_group - 1))

    for k in (0, 10, 11, *range(1, 10)):
        loads[k].start()

    below = my_slab + (my_row + 1) * (my_side + 1) - 1
    due = jnp.where(keeps, below * inner_group, below + 1)

    @pl.when((due > 0) | last)
    def _():
        pl.semaphore_wait(barrier, jnp.where(last, n - 1, due))


    @pl.when(keeps)
    def _():
        def tell_column(o, device):
            for core in range(inner_group):
                signal(column.at[o], (device[0], device[1] - my_core + core))

        def tell_plane(block, device):
            for core in range(inner_group):
                signal(known.at[0], (device[0], device[1] - my_core + core))

        when_slabs(tell_column, behind, up_slab)
        when_places(tell_plane, behind, up_row, up_side)

    @pl.when(last)
    def _():
        each_other(lambda block, device: signal(known.at[1], device), ahead_of)

    table_rows = pl.ds(0, nv + 1)
    loads[10].wait()
    loads[11].wait()

    def share(block, device):
        into = tables.at[block * inner_group + my_core, table_rows]
        remote(own.at[table_rows], into, 0, keeper_of(device))

    def share_down(block, o, i):
        @pl.when((my_row >= o) & (my_side >= i))
        def _():
            back = ((inner_clump - o) % inner_clump) * outer_group + (outer_group - i) % outer_group
            share(back, place(behind, o, i, 0, 0))

    offsets(share_down, inner_clump, outer_group, far_first=True)

    @pl.when(jnp.logical_not(keeps))
    def _():
        share(0, (my_clump, my_group))

    loads[0].wait()
    target = target_ref[...]
    owner, local = split_by(target, cells)
    owner_b = jnp.broadcast_to(owner.astype(F32), (cells, cells))
    same = owner_b == owner_b.T
    earlier = iota((cells, cells), 0) < iota((cells, cells), 1)
    rank = jnp.sum(jnp.where(same & earlier, 1.0, 0.0), axis=0, keepdims=True).astype(jnp.int32)
    to_clump, to_group = split_by(owner, n_group)
    to_slab, to_row = split_by(to_clump, inner_clump)
    to_side, to_core = split_by(to_group, inner_group)
    table = behind(my_row, to_row, inner_clump) * outer_group
    table = table + behind(my_side, to_side, outer_group)
    entry = table * inner_group + to_core
    slab = behind(to_slab, my_slab, outer_clump)
    wanted = (local + 1).astype(F32)
    asks = jnp.where(iota((outer_clump, cells), 0) == slab, wanted, 0.0).astype(BF16)
    ask_rows = dot_nt(asks, onehot(iota((128, cells), 0) == entry * slots + rank))
    for k in range(outer_clump):
        ask[k, 0:1, :] = ask_rows[k : k + 1]
    one_row = pl.ds(0, 1)

    def request(step, device):
        into = asked.at[step * inner_group + my_core, one_row]
        remote(ask.at[step, one_row], into, 1, keeper_of(device))

    @pl.when(jnp.logical_not(keeps))
    def _():
        request(0, (my_clump, my_group))

    def request_down(o):
        @pl.when(my_slab >= o)
        def _():
            request(outer_clump - o, place(behind, 0, 0, o, 0))

    slabs(request_down)

    frac = frac_ref[...]
    block = behind(to_row, my_row, inner_clump) * outer_group
    block = (block + behind(to_side, my_side, outer_group)) * outer_clump + slab
    block = (block * inner_group + behind(to_core, my_core, inner_group)) * stride
    part, line = split_by(rank, half)
    slot_of = onehot(iota((2 * rows, cells), 0) == part * rows + block + line)
    asks = jnp.where(iota((rows, cells), 0) == block, wanted, 0.0).astype(BF16)
    id_rows = dot_nt(asks, onehot(iota((128, cells), 0) == rank))
    in_stride = split_by(iota((rows, 128), 0), stride)[1]
    note[...] = jnp.where(in_stride == 1, jnp.broadcast_to(frac, (rows, cells)), id_rows)
    noted[0:2, :] = note[0:2, :]

    def lines_of(block, count):
        start = block * stride
        return pl.ds(start if isinstance(start, int) else pl.multiple_of(start, stride), count)

    def give_note(block, device):
        its = lines_of(block, 2)
        remote(note.at[its], noted.at[its], 4, device)

    @pl.when(last_place & last_plane)
    def _():
        @pl.when(jnp.logical_not(last))
        def _():
            pl.semaphore_wait(known.at[1], 1)

        each_other(give_note, ahead_of)


    for load in loads[1:10]:
        load.wait()
    lu_hi, lu_lo = halves(lwt_ref[...])
    lu_rows = rows_of([lu_hi, lu_lo, lgrid_ref[...]], 16)
    lu_of = onehot(iota((lus, cols), 0) == clu_ref[...])
    col_vals = dot(lu_rows, lu_of)
    col_w = cwt_ref[...] * (col_vals[0:1] + col_vals[1:2])

    c_hi, c_lo = halves(col_w)
    col_rows = rows_of([c_hi, c_lo, col_vals[2:3]], 16)
    col_of = onehot(iota((cols, patches), 0) == pcol_ref[...])
    patch_vals = dot(col_rows, col_of)
    alive = jnp.where(iota((1, patches), 1) < count_ref[0], 1.0, 0.0)
    weight = alive * pwt_ref[...] * (patch_vals[0:1] + patch_vals[1:2])
    home = patch_vals[2:3].astype(jnp.int32)
    home_of = onehot(iota((cells, patches), 0) == home)

    scales = scale_ref[...]
    t1 = scales.astype(BF16).astype(F32)
    t2 = (scales - t1).astype(BF16).astype(F32)
    t3 = scales - t1 - t2
    pad = 128 - 3 * types
    stacked = jnp.concatenate([t1, t2, t3, jnp.zeros((pad, nv), F32)], axis=0)
    stacked = jnp.concatenate([stacked, jnp.zeros((128, 128 - nv), F32)], axis=1)
    scale_t = stacked.T[:nv].astype(BF16)
    kind = iota((128, patches), 0)
    type_of = onehot(
        (kind == pft_ref[...])
        | (kind == pft_ref[...] + types)
        | (kind == pft_ref[...] + 2 * types)
    )
    scaled = flux_ref[...] * dot(scale_t, type_of)

    x_hi, x_lo = halves(scaled * weight)
    w_hi, w_lo = halves(weight)
    sums = dot_nt(
        jnp.concatenate([x_hi, x_lo, rows_of([w_hi, w_lo], 16)], axis=0), home_of
    )
    num = sums[:nv] + sums[nv : 2 * nv]
    den = sums[2 * nv : 2 * nv + 1] + sums[2 * nv + 1 : 2 * nv + 2]
    mean = num / jnp.maximum(den, 1.0)

    send[...] = pack(slot_of, mean)
    recv[0:half, :] = send[0:half, :]
    later = (up_row + 1) * (up_side + 1) - 1

    @pl.when(later > 0)
    def _():
        pl.semaphore_wait(known.at[0], later)

    def share_rest(block, o, i):
        row, side = ahead_of(my_row, o, inner_clump), ahead_of(my_side, i, outer_group)

        @pl.when((row > my_row) | (side > my_side))
        def _():
            share(block, place(ahead_of, o, i, 0, 0))

    offsets(share_rest, inner_clump, outer_group)

    def request_up(o):
        @pl.when(up_slab >= o)
        def _():
            pl.semaphore_wait(column.at[o], 1)
            request(o, place(ahead_of, 0, 0, o, 0))

    slabs(request_up)

    @pl.when(jnp.logical_not(last_place & last_plane))
    def _():
        pl.semaphore_wait(known.at[1], 1)
        each_other(give_note, ahead_of)

    def give(block, device):
        its = lines_of(block, half)
        remote(send.at[its], recv.at[its], 2, device)

    each_other(give, ahead_of)

    @pl.when(keeps)
    def _():
        wait(tables.at[pl.ds(0, sharers - 1), table_rows], recv_sem.at[0])
        held = [own if t == keeper else tables.at[t] for t in range(sharers)]
        held = [(1.0 - x[nv : nv + 1, :]) * x[0:nv, :] for x in held]
        held = [wide(held[2 * p], held[2 * p + 1]) for p in range(pairs)]

        asked[keeper, 0:1, :] = ask[0, 0:1, :]
        wait(asked.at[pl.ds(0, askers - 1), one_row], recv_sem.at[1])
        told = jnp.broadcast_to(asked[:, 0:1, :], (askers, slots, 128)).reshape(askers * slots, 128)
        lane_less = iota((askers * slots, 128), 1) - split_by(iota((askers * slots, 128), 0), slots)[1]
        spread = [jnp.where(lane_less == t * slots, told, 0.0) for t in range(sharers)]
        ids = dot(jnp.concatenate(spread, axis=0).astype(BF16), jnp.ones((128, cells), BF16))
        held_of = onehot(ids == (iota(ids.shape, 1) + 1).astype(F32))
        for p in range(pairs):
            one, two = 2 * p * askers * slots, (2 * p + 1) * askers * slots
            packed = pack_wide(held_of[one : two + askers * slots], held[p])
            reply[:, p * slots : (p + 1) * slots, :] = packed.reshape(askers, slots, 128)

        def respond(block, o, i):
            clump, group = place(behind, 0, 0, o, 0)
            remote(reply.at[block], back.at[o], 3, (clump, group - my_core + i))

        if outer_clump <= 8:
            for o in range(outer_clump - 1, -1, -1):
                for i in range(inner_group):
                    if o or i < keeper:
                        respond(o * inner_group + i, o, i)
        else:
            for i in range(keeper):
                respond(i, 0, i)

            @pl.loop(1, outer_clump)
            def _(o):
                for i in range(inner_group):
                    respond(o * inner_group + i, o, i)

        back[0] = reply[keeper]

    other = (1.0 - frac) * field_ref[...]
    pair, side = split_by(entry, 2)
    answers = outer_clump * pairs * slots
    spot = side * answers + (slab * pairs + pair) * slots + rank
    answer_of = onehot(iota((2 * answers, cells), 0) == spot)
    patch_of = (dot(answer_of, home_of) * alive).astype(BF16)

    flat = pl.ds(0, (n - 1) * half)
    keeps_or_not = ((keeps, 1), (jnp.logical_not(keeps), 0))
    for which, first in keeps_or_not:

        @pl.when(which)
        def _(first=first):
            wait(tables.at[pl.ds(0, places - first), table_rows], send_sem.at[0])
            wait(ask.at[pl.ds(0, outer_clump - first), one_row], send_sem.at[1])

    wait(send.at[flat], send_sem.at[2])
    wait(note.at[pl.ds(0, (n - 1) * 2)], send_sem.at[4])
    wait(noted.at[pl.ds(0, (n - 1) * 2)], recv_sem.at[4])
    lane = iota((2 * rows, 128), 0)
    lane_part = jnp.where(lane >= rows, 1, 0)
    lane_line = split_by(lane - lane_part * rows, stride)[1]
    its_lane = (lane_line < half) & (
        iota((2 * rows, 128), 1) == lane_part * half + lane_line
    )
    told = jnp.where(in_stride < 2, noted[...], 0.0)
    ids_of = jnp.broadcast_to(told.reshape(n, stride, 128)[:, 0:1, :], (n, stride, 128)).reshape(rows, 128)
    spread = jnp.where(its_lane, jnp.concatenate([ids_of, ids_of], axis=0), 0.0).astype(BF16)
    ids = dot(spread, jnp.ones((128, cells), BF16))
    owned_of = onehot(ids == (iota((2 * rows, cells), 1) + 1).astype(F32))

    back_of = (table * outer_clump + behind(my_slab, to_slab, outer_clump)) * inner_group
    back_of = (back_of + behind(my_core, to_core, inner_group)) * stride + 1
    all_frac = select(told.T, onehot(iota((rows, cells), 0) == back_of))
    cell_frac = jnp.sum(
        jnp.where(iota((128, cells), 0) == local, all_frac, 0.0), axis=0, keepdims=True
    )
    base = alive * (scaled - select(cell_frac * mean, home_of))

    @pl.when(keeps)
    def _():
        wait(reply.at[pl.ds(0, askers - 1)], send_sem.at[3])

    wait(recv.at[flat], recv_sem.at[2])
    in_half = split_by(iota((rows, 128), 0), stride)[1] < half
    owned = select(unpack(jnp.where(in_half, recv[...], 0.0)), owned_of)
    merged_ref[...] = frac * owned + other

    for which, first in keeps_or_not:

        @pl.when(which)
        def _(first=first):
            wait(back.at[pl.ds(first, outer_clump - first)], recv_sem.at[3])

    anomaly_ref[...] = base - select(unpack(back[...].reshape(answers, 128)), patch_of)


def store_kernel(merged, anomaly, merged_out, anomaly_out, sem):
    stores = [
        pltpu.make_async_copy(merged, merged_out, sem.at[0]),
        pltpu.make_async_copy(anomaly, anomaly_out, sem.at[1]),
    ]
    for store in stores:
        store.start()
    for store in stores:
        store.wait()


def per_device(
    flux, patch_pft, patch_wt, patch_col, col_wt, col_lu, lu_wt, lu_grid, cell_target,
    patch_count, pft_scale, cpl_frac, cpl_field,
):
    n_clump = lax.axis_size("clump")
    n_group = lax.axis_size("grp")
    n = n_clump * n_group
    nv = flux.shape[2]
    patches = flux.shape[1]
    cells = cell_target.shape[1]
    inner_group = 2 if n_group % 2 == 0 else 1
    outer_group = n_group // inner_group
    inner_clump = outer_group if n_clump % outer_group == 0 else 1
    sharers = inner_clump * n_group
    outer_clump = n_clump // inner_clump
    askers = outer_clump * inner_group
    cap = max(2, 2 * cells // n)
    half = -(-cap // 2)
    slots = -(-cap // 8) * 8
    stride = -(-half // 8) * 8
    vmem = pl.BlockSpec(memory_space=pltpu.VMEM)
    hbm = pl.BlockSpec(memory_space=pltpu.HBM)
    staged = (
        cell_target, lu_wt, lu_grid, col_lu, col_wt, patch_col, patch_wt,
        pft_scale, patch_pft, flux[0].T,
    )
    inputs = (*staged, cpl_frac.reshape(1, -1), cpl_field.T)
    shapes = (
        jax.ShapeDtypeStruct((nv, cells), F32),
        jax.ShapeDtypeStruct((nv, patches), F32),
    )
    results = pl.pallas_call(
        functools.partial(
            kernel, n_clump, n_group, inner_clump, inner_group, cap, slots, half, stride
        ),
        out_shape=tuple(pltpu.VMEM(x.shape, x.dtype) for x in shapes),
        in_specs=[pl.BlockSpec(memory_space=pltpu.SMEM)] + [hbm] * INPUTS,
        out_specs=(vmem, vmem),
        scratch_shapes=[
            pltpu.VMEM((sharers, -(-(nv + 1) // 8) * 8, cells), F32),
            pltpu.VMEM((-(-(nv + 1) // 8) * 8, cells), F32),
            pltpu.VMEM((outer_clump, 8, 128), F32),
            pltpu.VMEM((askers, 8, 128), F32),
            pltpu.VMEM((n * stride, 128), F32),
            pltpu.VMEM((n * stride, 128), F32),
            pltpu.VMEM((askers, sharers // 2 * slots, 128), F32),
            pltpu.VMEM((outer_clump, sharers // 2 * slots, 128), F32),
            pltpu.VMEM((n * stride, 128), F32),
            pltpu.VMEM((n * stride, 128), F32),
            pltpu.SemaphoreType.DMA((5,)),
            pltpu.SemaphoreType.DMA((5,)),
            pltpu.SemaphoreType.DMA((INPUTS,)),
            pltpu.SemaphoreType.REGULAR((2,)),
            pltpu.SemaphoreType.REGULAR((outer_clump,)),
        ]
        + [pltpu.VMEM(x.shape, x.dtype) for x in staged],
        compiler_params=pltpu.CompilerParams(
            collective_id=0, has_side_effects=True, vmem_limit_bytes=48 * 1024 * 1024
        ),
    )(patch_count, *[pltpu.with_memory_space_constraint(x, pltpu.HBM) for x in inputs])
    merged, anomaly = pl.pallas_call(
        store_kernel,
        out_shape=shapes,
        in_specs=[vmem, vmem],
        out_specs=(hbm, hbm),
        scratch_shapes=[pltpu.SemaphoreType.DMA((2,))],
        compiler_params=pltpu.CompilerParams(vmem_limit_bytes=4 * 1024 * 1024),
    )(*results)
    return merged.T, anomaly.T[None]


def solution(mesh):
    split = P(("clump", "grp"))
    return jax.shard_map(
        per_device,
        mesh=mesh,
        in_specs=(split,) * 10 + (P(),) + (split,) * 2,
        out_specs=(split, split),
        check_vma=False,
    )
```

time: 16 us -> 14.8 us (0.925)
  the two profiles are of different devices: /device:TPU:0 before, /device:TPU:3 now
where the time goes in v2:
time: 14.8 us; the launch traced here: 14.6 us
  Pallas kernels  13.3 us (90%)
  between operations  1.29 us (9%)
    pallas_call x1, Pallas kernels, per_device(): pl.pallas_call(functools.partial(kernel, n_clump, n_group, inner_clump, i...  12.6 us
    pallas_call x1, Pallas kernels, per_device(): pl.pallas_call(store_kernel, out_shape=shapes, in_specs=[vmem, vmem], out...  0.73 us

profile of v2, /device:TPU:3, one launch (start us, length us, event | category | flops | bytes accessed | tf_op | source)
XLA Modules:
  0.0 14.6 jit_solution(17411326194597206542)
XLA Ops:
  1.3 12.6 %shard_map.140 = (f32[64,128]{1,0:T(8,128)S(1)}, f32[64,1024]{1,0:T(8,128)S(1)}) custom-call(s32[1]{0:T(128)S(6)} %copy.15.refs_0_, s32[1,128]{1,0:T(1,128)} %refs_1_.1, f32[1,256]{1,0:T(1,128)} %refs_2_.1, s32[1,256]{1,0:T(1,128)} %refs_3_.1, s32[1,512]{1,0:T(1,128)} %refs_4_.1, f32[1,512]{1,0:T(1,128)} %refs_5_.1, s32[1,1024]{1,0:T(1,128)} %refs_6_.1, ...), custom_call_target="tpu_custom_call" | custom-call | tf_op jit(solution)/shard_map/pallas_call | solution.py:556
  13.9 0.7 %shard_map.141 = (f32[64,128]{1,0:T(8,128)}, f32[64,1024]{1,0:T(8,128)}) custom-call(f32[64,128]{1,0:T(8,128)S(1)} %get-tuple-element.6.merged, f32[64,1024]{1,0:T(8,128)S(1)} %get-tuple-element.7.anomaly), custom_call_target="tpu_custom_call" | custom-call | tf_op jit(solution)/shard_map/pallas_call | solution.py:585

commit v3 on v2

--- a/solution.py
+++ b/solution.py
@@ -90,8 +90,8 @@
     sources, refs = refs[:INPUTS], refs[INPUTS:]
     merged_ref, anomaly_ref = refs[:2]
     tables, own, ask, asked, note, noted, reply, back, send, recv = refs[2:12]
-    send_sem, recv_sem, in_sem, known, column = refs[12:17]
-    staged = refs[17:]
+    send_sem, recv_sem, in_sem, known = refs[12:16]
+    staged = refs[16:]
     (
         target_ref, lwt_ref, lgrid_ref, clu_ref, cwt_ref, pcol_ref, pwt_ref,
         scale_ref, pft_ref, flux_ref,
@@ -109,7 +109,7 @@
     pairs = sharers // 2
     field_ref, frac_ref = own.at[pl.ds(0, nv)], own.at[pl.ds(nv, 1)]
     loads = [
-        pltpu.make_async_copy(source, into, in_sem.at[k])
+        pltpu.make_async_copy(source, into, in_sem.at[0 if k == 0 else 2 if k < 10 else 1])
         for k, (source, into) in enumerate(zip(sources, (*staged, frac_ref, field_ref)))
     ]
     my_clump, my_group = lax.axis_index("clump"), lax.axis_index("grp")
@@ -156,10 +156,11 @@
                 offsets(one, outer_clump, inner_group, own=t > 0)
 
     def remote(source, into, k, device):
+        sent = 1 if k == 3 else 0
         pltpu.make_async_remote_copy(
             src_ref=source,
             dst_ref=into,
-            send_sem=send_sem.at[k],
+            send_sem=send_sem.at[sent],
             recv_sem=recv_sem.at[k],
             device_id=device,
             device_id_type=MESH,
@@ -173,13 +174,11 @@
     def signal(sem, device):
         pl.semaphore_signal(sem, inc=1, device_id=device, device_id_type=MESH)
 
-    def when_places(act, there, first, second):
+    def each_place(act, there):
         def one(block, o, i):
-            @pl.when((first + o < inner_clump) & (second + i < outer_group))
-            def _():
-                act(block, place(there, o, i, 0, 0))
-
-        offsets(one, inner_clump, outer_group)
+            act(block, place(there, o, i, 0, 0))
+
+        offsets(one, inner_clump, outer_group, far_first=True)
 
     def slabs(act):
         if outer_clump <= 8:
@@ -188,90 +187,61 @@
         else:
             pl.loop(1, outer_clump)(act)
 
-    def when_slabs(act, there, first):
-        def one(o):
-            @pl.when(first + o < outer_clump)
-            def _():
-                act(o, place(there, 0, 0, o, 0))
-
-        slabs(one)
+    def each_slab(act, there):
+        slabs(lambda o: act(o, place(there, 0, 0, o, 0)))
+
+    def core_of(device, core):
+        return device[0], device[1] - my_core + core
 
     def keeper_of(device):
-        return device[0], device[1] - my_core + keeper
-
-    def greet(block, device):
-        signal(barrier, keeper_of(device))
-
-        @pl.when(keeps)
-        def _():
-            for core in range(keeper):
-                signal(barrier, (device[0], device[1] - my_core + core))
-
-    up_row, up_side = inner_clump - 1 - my_row, outer_group - 1 - my_side
-    up_slab = outer_clump - 1 - my_slab
-    last_place, last_plane = up_row + up_side == 0, up_slab == 0
-    last = last_place & last_plane & keeps
-    when_slabs(greet, ahead_of, my_slab)
-    when_places(greet, ahead_of, my_row, my_side)
-    mates = [(my_clump, my_group - my_core + core) for core in range(inner_group)]
+        return core_of(device, keeper)
+
+    here = (my_clump, my_group)
+    last_place = (my_row == inner_clump - 1) & (my_side == outer_group - 1)
+    last_plane = my_slab == outer_clump - 1
+    last_chip = last_place & last_plane
+    last = last_chip & keeps
+
+    def greet(step, device):
+        for core in range(inner_group):
+            signal(barrier, core_of(device, core))
 
     @pl.when(keeps)
     def _():
+        each_slab(greet, ahead_of)
+        each_place(greet, ahead_of)
         for core in range(keeper):
-            signal(barrier, mates[core])
-
-    @pl.when((last_place == last_plane) & jnp.logical_not(last))
+            signal(barrier, core_of(here, core))
+
+    @pl.when(jnp.logical_not(keeps & (last_place | last_plane)))
     def _():
         signal(barrier, (n_clump - 1, n_group - 1))
 
     for k in (0, 10, 11, *range(1, 10)):
         loads[k].start()
 
-    below = my_slab + (my_row + 1) * (my_side + 1) - 1
-    due = jnp.where(keeps, below * inner_group, below + 1)
-
-    @pl.when((due > 0) | last)
-    def _():
-        pl.semaphore_wait(barrier, jnp.where(last, n - 1, due))
-
-
-    @pl.when(keeps)
-    def _():
-        def tell_column(o, device):
-            for core in range(inner_group):
-                signal(column.at[o], (device[0], device[1] - my_core + core))
-
-        def tell_plane(block, device):
-            for core in range(inner_group):
-                signal(known.at[0], (device[0], device[1] - my_core + core))
-
-        when_slabs(tell_column, behind, up_slab)
-        when_places(tell_plane, behind, up_row, up_side)
-
-    @pl.when(last)
-    def _():
-        each_other(lambda block, device: signal(known.at[1], device), ahead_of)
-
     table_rows = pl.ds(0, nv + 1)
-    loads[10].wait()
-    loads[11].wait()
 
     def share(block, device):
         into = tables.at[block * inner_group + my_core, table_rows]
         remote(own.at[table_rows], into, 0, keeper_of(device))
 
-    def share_down(block, o, i):
-        @pl.when((my_row >= o) & (my_side >= i))
+    def enter():
+        loads[10].wait()
+        loads[11].wait()
+        near = outer_clump + places - 2 + jnp.where(keeps, 0, 1)
+        pl.semaphore_wait(barrier, jnp.where(last, n - 1, near))
+        each_place(share, ahead_of)
+
+        @pl.when(jnp.logical_not(keeps))
         def _():
-            back = ((inner_clump - o) % inner_clump) * outer_group + (outer_group - i) % outer_group
-            share(back, place(behind, o, i, 0, 0))
-
-    offsets(share_down, inner_clump, outer_group, far_first=True)
-
-    @pl.when(jnp.logical_not(keeps))
-    def _():
-        share(0, (my_clump, my_group))
-
+            share(0, here)
+
+        @pl.when(last)
+        def _():
+            each_other(lambda block, device: signal(known, device), ahead_of)
+
+    pl.when(last_chip)(enter)
     loads[0].wait()
     target = target_ref[...]
     owner, local = split_by(target, cells)
@@ -292,6 +262,7 @@
     for k in range(outer_clump):
         ask[k, 0:1, :] = ask_rows[k : k + 1]
     one_row = pl.ds(0, 1)
+    pl.when(jnp.logical_not(last_chip))(enter)
 
     def request(step, device):
         into = asked.at[step * inner_group + my_core, one_row]
@@ -299,15 +270,9 @@
 
     @pl.when(jnp.logical_not(keeps))
     def _():
-        request(0, (my_clump, my_group))
-
-    def request_down(o):
-        @pl.when(my_slab >= o)
-        def _():
-            request(outer_clump - o, place(behind, 0, 0, o, 0))
-
-    slabs(request_down)
-
+        request(0, here)
+
+    each_slab(request, ahead_of)
     frac = frac_ref[...]
     block = behind(to_row, my_row, inner_clump) * outer_group
     block = (block + behind(to_side, my_side, outer_group)) * outer_clump + slab
@@ -328,11 +293,11 @@
         its = lines_of(block, 2)
         remote(note.at[its], noted.at[its], 4, device)
 
-    @pl.when(last_place & last_plane)
+    @pl.when(last_chip)
     def _():
         @pl.when(jnp.logical_not(last))
         def _():
-            pl.semaphore_wait(known.at[1], 1)
+            pl.semaphore_wait(known, 1)
 
         each_other(give_note, ahead_of)
 
@@ -381,32 +346,9 @@
 
     send[...] = pack(slot_of, mean)
     recv[0:half, :] = send[0:half, :]
-    later = (up_row + 1) * (up_side + 1) - 1
-
-    @pl.when(later > 0)
-    def _():
-        pl.semaphore_wait(known.at[0], later)
-
-    def share_rest(block, o, i):
-        row, side = ahead_of(my_row, o, inner_clump), ahead_of(my_side, i, outer_group)
-
-        @pl.when((row > my_row) | (side > my_side))
-        def _():
-            share(block, place(ahead_of, o, i, 0, 0))
-
-    offsets(share_rest, inner_clump, outer_group)
-
-    def request_up(o):
-        @pl.when(up_slab >= o)
-        def _():
-            pl.semaphore_wait(column.at[o], 1)
-            request(o, place(ahead_of, 0, 0, o, 0))
-
-    slabs(request_up)
-
-    @pl.when(jnp.logical_not(last_place & last_plane))
-    def _():
-        pl.semaphore_wait(known.at[1], 1)
+    @pl.when(jnp.logical_not(last_chip))
+    def _():
+        pl.semaphore_wait(known, 1)
         each_other(give_note, ahead_of)
 
     def give(block, device):
@@ -417,11 +359,6 @@
 
     @pl.when(keeps)
     def _():
-        wait(tables.at[pl.ds(0, sharers - 1), table_rows], recv_sem.at[0])
-        held = [own if t == keeper else tables.at[t] for t in range(sharers)]
-        held = [(1.0 - x[nv : nv + 1, :]) * x[0:nv, :] for x in held]
-        held = [wide(held[2 * p], held[2 * p + 1]) for p in range(pairs)]
-
         asked[keeper, 0:1, :] = ask[0, 0:1, :]
         wait(asked.at[pl.ds(0, askers - 1), one_row], recv_sem.at[1])
         told = jnp.broadcast_to(asked[:, 0:1, :], (askers, slots, 128)).reshape(askers * slots, 128)
@@ -429,6 +366,11 @@
         spread = [jnp.where(lane_less == t * slots, told, 0.0) for t in range(sharers)]
         ids = dot(jnp.concatenate(spread, axis=0).astype(BF16), jnp.ones((128, cells), BF16))
         held_of = onehot(ids == (iota(ids.shape, 1) + 1).astype(F32))
+
+        wait(tables.at[pl.ds(0, sharers - 1), table_rows], recv_sem.at[0])
+        held = [own if t == keeper else tables.at[t] for t in range(sharers)]
+        held = [(1.0 - x[nv : nv + 1, :]) * x[0:nv, :] for x in held]
+        held = [wide(held[2 * p], held[2 * p + 1]) for p in range(pairs)]
         for p in range(pairs):
             one, two = 2 * p * askers * slots, (2 * p + 1) * askers * slots
             packed = pack_wide(held_of[one : two + askers * slots], held[p])
@@ -468,10 +410,10 @@
         @pl.when(which)
         def _(first=first):
             wait(tables.at[pl.ds(0, places - first), table_rows], send_sem.at[0])
-            wait(ask.at[pl.ds(0, outer_clump - first), one_row], send_sem.at[1])
-
-    wait(send.at[flat], send_sem.at[2])
-    wait(note.at[pl.ds(0, (n - 1) * 2)], send_sem.at[4])
+            wait(ask.at[pl.ds(0, outer_clump - first), one_row], send_sem.at[0])
+
+    wait(send.at[flat], send_sem.at[0])
+    wait(note.at[pl.ds(0, (n - 1) * 2)], send_sem.at[0])
     wait(noted.at[pl.ds(0, (n - 1) * 2)], recv_sem.at[4])
     lane = iota((2 * rows, 128), 0)
     lane_part = jnp.where(lane >= rows, 1, 0)
@@ -495,7 +437,7 @@
 
     @pl.when(keeps)
     def _():
-        wait(reply.at[pl.ds(0, askers - 1)], send_sem.at[3])
+        wait(reply.at[pl.ds(0, askers - 1)], send_sem.at[1])
 
     wait(recv.at[flat], recv_sem.at[2])
     in_half = split_by(iota((rows, 128), 0), stride)[1] < half
@@ -571,11 +513,10 @@
             pltpu.VMEM((outer_clump, sharers // 2 * slots, 128), F32),
             pltpu.VMEM((n * stride, 128), F32),
             pltpu.VMEM((n * stride, 128), F32),
+            pltpu.SemaphoreType.DMA((2,)),
             pltpu.SemaphoreType.DMA((5,)),
-            pltpu.SemaphoreType.DMA((5,)),
-            pltpu.SemaphoreType.DMA((INPUTS,)),
-            pltpu.SemaphoreType.REGULAR((2,)),
-            pltpu.SemaphoreType.REGULAR((outer_clump,)),
+            pltpu.SemaphoreType.DMA((3,)),
+            pltpu.SemaphoreType.REGULAR,
         ]
         + [pltpu.VMEM(x.shape, x.dtype) for x in staged],
         compiler_params=pltpu.CompilerParams(

time: 14.8 us -> 14.3 us (0.966)
  the two profiles are of different devices: /device:TPU:3 before, /device:TPU:0 now
where the time goes in v3:
time: 14.3 us; the launch traced here: 14.1 us
  Pallas kernels  12.8 us (90%)
  between operations  1.29 us (9%)
    pallas_call x1, Pallas kernels, per_device(): pl.pallas_call(functools.partial(kernel, n_clump, n_group, inner_clump, i...  12.1 us
    pallas_call x1, Pallas kernels, per_device(): pl.pallas_call(store_kernel, out_shape=shapes, in_specs=[vmem, vmem], out...  0.73 us

profile of v3, /device:TPU:0, one launch (start us, length us, event | category | flops | bytes accessed | tf_op | source)
XLA Modules:
  0.0 14.1 jit_solution(4417880435128871759)
XLA Ops:
  1.3 12.1 %shard_map.140 = (f32[64,128]{1,0:T(8,128)S(1)}, f32[64,1024]{1,0:T(8,128)S(1)}) custom-call(s32[1]{0:T(128)S(6)} %copy.15.refs_0_, s32[1,128]{1,0:T(1,128)} %refs_1_.1, f32[1,256]{1,0:T(1,128)} %refs_2_.1, s32[1,256]{1,0:T(1,128)} %refs_3_.1, s32[1,512]{1,0:T(1,128)} %refs_4_.1, f32[1,512]{1,0:T(1,128)} %refs_5_.1, s32[1,1024]{1,0:T(1,128)} %refs_6_.1, ...), custom_call_target="tpu_custom_call" | custom-call | tf_op jit(solution)/shard_map/pallas_call | solution.py:498
  13.4 0.7 %shard_map.141 = (f32[64,128]{1,0:T(8,128)}, f32[64,1024]{1,0:T(8,128)}) custom-call(f32[64,128]{1,0:T(8,128)S(1)} %get-tuple-element.6.merged, f32[64,1024]{1,0:T(8,128)S(1)} %get-tuple-element.7.anomaly), custom_call_target="tpu_custom_call" | custom-call | tf_op jit(solution)/shard_map/pallas_call | solution.py:526

commit v4 on v3

--- a/solution.py
+++ b/solution.py
@@ -88,10 +88,10 @@
 ):
     count_ref, *refs = refs
     sources, refs = refs[:INPUTS], refs[INPUTS:]
-    merged_ref, anomaly_ref = refs[:2]
-    tables, own, ask, asked, note, noted, reply, back, send, recv = refs[2:12]
-    send_sem, recv_sem, in_sem, known = refs[12:16]
-    staged = refs[16:]
+    merged_ref, base_ref, patch_of_ref, answers_ref = refs[:4]
+    tables, own, ask, asked, note, noted, reply, back, send, recv = refs[4:14]
+    send_sem, recv_sem, in_sem, known = refs[14:18]
+    staged = refs[18:]
     (
         target_ref, lwt_ref, lgrid_ref, clu_ref, cwt_ref, pcol_ref, pwt_ref,
         scale_ref, pft_ref, flux_ref,
@@ -401,7 +401,7 @@
     answers = outer_clump * pairs * slots
     spot = side * answers + (slab * pairs + pair) * slots + rank
     answer_of = onehot(iota((2 * answers, cells), 0) == spot)
-    patch_of = (dot(answer_of, home_of) * alive).astype(BF16)
+    patch_of_ref[...] = (dot(answer_of, home_of) * alive).astype(BF16)
 
     flat = pl.ds(0, (n - 1) * half)
     keeps_or_not = ((keeps, 1), (jnp.logical_not(keeps), 0))
@@ -433,7 +433,7 @@
     cell_frac = jnp.sum(
         jnp.where(iota((128, cells), 0) == local, all_frac, 0.0), axis=0, keepdims=True
     )
-    base = alive * (scaled - select(cell_frac * mean, home_of))
+    base_ref[...] = alive * (scaled - select(cell_frac * mean, home_of))
 
     @pl.when(keeps)
     def _():
@@ -450,16 +450,22 @@
         def _(first=first):
             wait(back.at[pl.ds(first, outer_clump - first)], recv_sem.at[3])
 
-    anomaly_ref[...] = base - select(unpack(back[...].reshape(answers, 128)), patch_of)
-
-
-def store_kernel(merged, anomaly, merged_out, anomaly_out, sem):
-    stores = [
-        pltpu.make_async_copy(merged, merged_out, sem.at[0]),
-        pltpu.make_async_copy(anomaly, anomaly_out, sem.at[1]),
-    ]
-    for store in stores:
-        store.start()
+    answers_ref[...] = back[...].reshape(answers, 128)
+
+
+def store_kernel(merged, base, patch_of, answers, merged_out, anomaly_out, anomaly, sem):
+    chunks = anomaly.shape[0]
+    width = anomaly.shape[2]
+    stores = [pltpu.make_async_copy(merged, merged_out, sem.at[chunks])]
+    stores[0].start()
+    high, low = halves(unpack(answers[...]))
+    table = jnp.concatenate([high, low], axis=0)
+    for k in range(chunks):
+        its = pl.ds(k * width, width)
+        both = dot(table, patch_of[:, its])
+        anomaly[k] = base[:, its] - (both[: high.shape[0]] + both[high.shape[0] :])
+        stores.append(pltpu.make_async_copy(anomaly.at[k], anomaly_out.at[:, its], sem.at[k]))
+        stores[-1].start()
     for store in stores:
         store.wait()
 
@@ -484,6 +490,8 @@
     half = -(-cap // 2)
     slots = -(-cap // 8) * 8
     stride = -(-half // 8) * 8
+    answers = outer_clump * (sharers // 2) * slots
+    chunks = 2
     vmem = pl.BlockSpec(memory_space=pltpu.VMEM)
     hbm = pl.BlockSpec(memory_space=pltpu.HBM)
     staged = (
@@ -499,9 +507,14 @@
         functools.partial(
             kernel, n_clump, n_group, inner_clump, inner_group, cap, slots, half, stride
         ),
-        out_shape=tuple(pltpu.VMEM(x.shape, x.dtype) for x in shapes),
+        out_shape=(
+            pltpu.VMEM((nv, cells), F32),
+            pltpu.VMEM((nv, patches), F32),
+            pltpu.VMEM((2 * answers, patches), BF16),
+            pltpu.VMEM((answers, 128), F32),
+        ),
         in_specs=[pl.BlockSpec(memory_space=pltpu.SMEM)] + [hbm] * INPUTS,
-        out_specs=(vmem, vmem),
+        out_specs=(vmem,) * 4,
         scratch_shapes=[
             pltpu.VMEM((sharers, -(-(nv + 1) // 8) * 8, cells), F32),
             pltpu.VMEM((-(-(nv + 1) // 8) * 8, cells), F32),
@@ -526,10 +539,13 @@
     merged, anomaly = pl.pallas_call(
         store_kernel,
         out_shape=shapes,
-        in_specs=[vmem, vmem],
+        in_specs=[vmem] * 4,
         out_specs=(hbm, hbm),
-        scratch_shapes=[pltpu.SemaphoreType.DMA((2,))],
-        compiler_params=pltpu.CompilerParams(vmem_limit_bytes=4 * 1024 * 1024),
+        scratch_shapes=[
+            pltpu.VMEM((chunks, nv, patches // chunks), F32),
+            pltpu.SemaphoreType.DMA((chunks + 1,)),
+        ],
+        compiler_params=pltpu.CompilerParams(vmem_limit_bytes=8 * 1024 * 1024),
     )(*results)
     return merged.T, anomaly.T[None]
 

time: 14.3 us -> 14.3 us (level)
    pallas_call x1, Pallas kernels: 12.1 us -> 11.8 us  [per_device(): pl.pallas_call(functools.partial(kernel, n_clump, n_group, inner_clump, i...]
    pallas_call x1, Pallas kernels: 0.73 us -> 0.97 us  [per_device(): pl.pallas_call(store_kernel, out_shape=shapes, in_specs=[vmem] * 4, out_s...]
where the time goes in v4:
time: 14.3 us; the launch traced here: 14.1 us
  Pallas kernels  12.8 us (90%)
  between operations  1.29 us (9%)
    pallas_call x1, Pallas kernels, per_device(): pl.pallas_call(functools.partial(kernel, n_clump, n_group, inner_clump, i...  11.8 us
    pallas_call x1, Pallas kernels, per_device(): pl.pallas_call(store_kernel, out_shape=shapes, in_specs=[vmem] * 4, out_s...  0.97 us

profile of v4, /device:TPU:0, one launch (start us, length us, event | category | flops | bytes accessed | tf_op | source)
XLA Modules:
  0.0 14.1 jit_solution(1169429357766488633)
XLA Ops:
  1.3 11.8 %shard_map.140 = (f32[64,128]{1,0:T(8,128)S(1)}, f32[64,1024]{1,0:T(8,128)S(1)}, bf16[256,1024]{1,0:T(8,128)(2,1)S(1)}, f32[128,128]{1,0:T(8,128)S(1)}) custom-call(s32[1]{0:T(128)S(6)} %copy.15.refs_0_, s32[1,128]{1,0:T(1,128)} %refs_1_.1, f32[1,256]{1,0:T(1,128)} %refs_2_.1, s32[1,256]{1,0:T(1,128)} %refs_3_.1, s32[1,512]{1,0:T(1,128)} %refs_4_.1, ...), custom_call_target="tpu_custom_call" | custom-call | tf_op jit(solution)/shard_map/pallas_call | solution.py:506
  13.1 1.0 %shard_map.141 = (f32[64,128]{1,0:T(8,128)}, f32[64,1024]{1,0:T(8,128)}) custom-call(f32[64,128]{1,0:T(8,128)S(1)} %get-tuple-element.8.merged, f32[64,1024]{1,0:T(8,128)S(1)} %get-tuple-element.9.base, bf16[256,1024]{1,0:T(8,128)(2,1)S(1)} %get-tuple-element.10.patch_of, f32[128,128]{1,0:T(8,128)S(1)} %get-tuple-element.11.answers), custom_call_target="tpu_custom_call" | custom-call | tf_op jit(solution)/shard_map/pallas_call | solution.py:539

commit v5 on v4

--- a/solution.py
+++ b/solution.py
@@ -89,9 +89,9 @@
     count_ref, *refs = refs
     sources, refs = refs[:INPUTS], refs[INPUTS:]
     merged_ref, base_ref, patch_of_ref, answers_ref = refs[:4]
-    tables, own, ask, asked, note, noted, reply, back, send, recv = refs[4:14]
-    send_sem, recv_sem, in_sem, known = refs[14:18]
-    staged = refs[18:]
+    tables, own, ask, asked, note, noted, fore, reply, back, send, recv = refs[4:15]
+    send_sem, recv_sem, in_sem, known = refs[15:19]
+    staged = refs[19:]
     (
         target_ref, lwt_ref, lgrid_ref, clu_ref, cwt_ref, pcol_ref, pwt_ref,
         scale_ref, pft_ref, flux_ref,
@@ -208,12 +208,16 @@
 
     @pl.when(keeps)
     def _():
-        each_slab(greet, ahead_of)
+        each_slab(lambda o, device: signal(barrier, keeper_of(device)), ahead_of)
         each_place(greet, ahead_of)
         for core in range(keeper):
             signal(barrier, core_of(here, core))
 
-    @pl.when(jnp.logical_not(keeps & (last_place | last_plane)))
+    @pl.when(jnp.logical_not(keeps))
+    def _():
+        signal(barrier, keeper_of(here))
+
+    @pl.when(jnp.logical_not(keeps & (last_place | last_plane) | last_chip))
     def _():
         signal(barrier, (n_clump - 1, n_group - 1))
 
@@ -229,9 +233,14 @@
     def enter():
         loads[10].wait()
         loads[11].wait()
-        near = outer_clump + places - 2 + jnp.where(keeps, 0, 1)
+        near = places - 1 + jnp.where(keeps, outer_clump - 1 + keeper, 1)
         pl.semaphore_wait(barrier, jnp.where(last, n - 1, near))
         each_place(share, ahead_of)
+
+        @pl.when(keeps)
+        def _():
+            for core in range(keeper):
+                signal(known.at[0], core_of(here, core))
 
         @pl.when(jnp.logical_not(keeps))
         def _():
@@ -239,7 +248,7 @@
 
         @pl.when(last)
         def _():
-            each_other(lambda block, device: signal(known, device), ahead_of)
+            each_other(lambda block, device: signal(known.at[1], device), ahead_of)
 
     pl.when(last_chip)(enter)
     loads[0].wait()
@@ -272,6 +281,10 @@
     def _():
         request(0, here)
 
+    @pl.when(jnp.logical_not(keeps))
+    def _():
+        pl.semaphore_wait(known.at[0], 1)
+
     each_slab(request, ahead_of)
     frac = frac_ref[...]
     block = behind(to_row, my_row, inner_clump) * outer_group
@@ -297,7 +310,7 @@
     def _():
         @pl.when(jnp.logical_not(last))
         def _():
-            pl.semaphore_wait(known, 1)
+            pl.semaphore_wait(known.at[1], 1)
 
         each_other(give_note, ahead_of)
 
@@ -348,7 +361,7 @@
     recv[0:half, :] = send[0:half, :]
     @pl.when(jnp.logical_not(last_chip))
     def _():
-        pl.semaphore_wait(known, 1)
+        pl.semaphore_wait(known.at[1], 1)
         each_other(give_note, ahead_of)
 
     def give(block, device):
@@ -361,39 +374,47 @@
     def _():
         asked[keeper, 0:1, :] = ask[0, 0:1, :]
         wait(asked.at[pl.ds(0, askers - 1), one_row], recv_sem.at[1])
-        told = jnp.broadcast_to(asked[:, 0:1, :], (askers, slots, 128)).reshape(askers * slots, 128)
-        lane_less = iota((askers * slots, 128), 1) - split_by(iota((askers * slots, 128), 0), slots)[1]
-        spread = [jnp.where(lane_less == t * slots, told, 0.0) for t in range(sharers)]
-        ids = dot(jnp.concatenate(spread, axis=0).astype(BF16), jnp.ones((128, cells), BF16))
-        held_of = onehot(ids == (iota(ids.shape, 1) + 1).astype(F32))
-
+
+        def picks(told, count):
+            height = count * slots
+            told = jnp.broadcast_to(told, (count, slots, 128)).reshape(height, 128)
+            lane_less = iota((height, 128), 1) - split_by(iota((height, 128), 0), slots)[1]
+            spread = [jnp.where(lane_less == t * slots, told, 0.0) for t in range(sharers)]
+            ids = dot(jnp.concatenate(spread, axis=0).astype(BF16), jnp.ones((128, cells), BF16))
+            return onehot(ids == (iota(ids.shape, 1) + 1).astype(F32))
+
+        def fill(into, chosen, count):
+            for p in range(pairs):
+                one, end = 2 * p * count * slots, 2 * (p + 1) * count * slots
+                packed = pack_wide(chosen[one:end], held[p])
+                into[:, p * slots : (p + 1) * slots, :] = packed.reshape(count, slots, 128)
+
+        first = pl.ds(my_slab * inner_group, inner_group)
+        first_picks = picks(asked[first, 0:1, :], inner_group)
         wait(tables.at[pl.ds(0, sharers - 1), table_rows], recv_sem.at[0])
         held = [own if t == keeper else tables.at[t] for t in range(sharers)]
         held = [(1.0 - x[nv : nv + 1, :]) * x[0:nv, :] for x in held]
         held = [wide(held[2 * p], held[2 * p + 1]) for p in range(pairs)]
-        for p in range(pairs):
-            one, two = 2 * p * askers * slots, (2 * p + 1) * askers * slots
-            packed = pack_wide(held_of[one : two + askers * slots], held[p])
-            reply[:, p * slots : (p + 1) * slots, :] = packed.reshape(askers, slots, 128)
-
-        def respond(block, o, i):
+        fill(fore, first_picks, inner_group)
+        for i in range(inner_group):
+
+            @pl.when((my_slab > 0) | (i < keeper))
+            def _(i=i):
+                remote(fore.at[i], back.at[my_slab], 3, (my_row, my_group - my_core + i))
+
+        fill(reply, picks(asked[:, 0:1, :], askers), askers)
+
+        def respond(o):
             clump, group = place(behind, 0, 0, o, 0)
-            remote(reply.at[block], back.at[o], 3, (clump, group - my_core + i))
-
-        if outer_clump <= 8:
-            for o in range(outer_clump - 1, -1, -1):
-                for i in range(inner_group):
-                    if o or i < keeper:
-                        respond(o * inner_group + i, o, i)
-        else:
-            for i in range(keeper):
-                respond(i, 0, i)
-
-            @pl.loop(1, outer_clump)
-            def _(o):
-                for i in range(inner_group):
-                    respond(o * inner_group + i, o, i)
-
+            for i in range(keeper if isinstance(o, int) and o == 0 else inner_group):
+                source = reply.at[o * inner_group + i]
+                remote(source, back.at[o], 3, (clump, group - my_core + i))
+
+        def respond_rest(o):
+            pl.when(my_slab != o)(lambda: respond(o))
+
+        respond_rest(0)
+        slabs(respond_rest)
         back[0] = reply[keeper]
 
     other = (1.0 - frac) * field_ref[...]
@@ -522,6 +543,7 @@
             pltpu.VMEM((askers, 8, 128), F32),
             pltpu.VMEM((n * stride, 128), F32),
             pltpu.VMEM((n * stride, 128), F32),
+            pltpu.VMEM((inner_group, sharers // 2 * slots, 128), F32),
             pltpu.VMEM((askers, sharers // 2 * slots, 128), F32),
             pltpu.VMEM((outer_clump, sharers // 2 * slots, 128), F32),
             pltpu.VMEM((n * stride, 128), F32),
@@ -529,7 +551,7 @@
             pltpu.SemaphoreType.DMA((2,)),
             pltpu.SemaphoreType.DMA((5,)),
             pltpu.SemaphoreType.DMA((3,)),
-            pltpu.SemaphoreType.REGULAR,
+            pltpu.SemaphoreType.REGULAR((2,)),
         ]
         + [pltpu.VMEM(x.shape, x.dtype) for x in staged],
         compiler_params=pltpu.CompilerParams(

time: 14.3 us -> 14.1 us (0.986)
  Pallas kernels: 12.8 us -> 12.6 us
    pallas_call x1, Pallas kernels: 11.8 us -> 11.6 us  [per_device(): pl.pallas_call(functools.partial(kernel, n_clump, n_group, inner_clump, i...]
where the time goes in v5:
time: 14.1 us; the launch traced here: 13.9 us
  Pallas kernels  12.6 us (89%)
  between operations  1.29 us (9%)
    pallas_call x1, Pallas kernels, per_device(): pl.pallas_call(functools.partial(kernel, n_clump, n_group, inner_clump, i...  11.6 us
    pallas_call x1, Pallas kernels, per_device(): pl.pallas_call(store_kernel, out_shape=shapes, in_specs=[vmem] * 4, out_s...  0.97 us

profile of v5, /device:TPU:0, one launch (start us, length us, event | category | flops | bytes accessed | tf_op | source)
XLA Modules:
  0.0 13.9 jit_solution(14402226776438855633)
XLA Ops:
  1.3 11.6 %shard_map.140 = (f32[64,128]{1,0:T(8,128)S(1)}, f32[64,1024]{1,0:T(8,128)S(1)}, bf16[256,1024]{1,0:T(8,128)(2,1)S(1)}, f32[128,128]{1,0:T(8,128)S(1)}) custom-call(s32[1]{0:T(128)S(6)} %copy.15.refs_0_, s32[1,128]{1,0:T(1,128)} %refs_1_.1, f32[1,256]{1,0:T(1,128)} %refs_2_.1, s32[1,256]{1,0:T(1,128)} %refs_3_.1, s32[1,512]{1,0:T(1,128)} %refs_4_.1, ...), custom_call_target="tpu_custom_call" | custom-call | tf_op jit(solution)/shard_map/pallas_call | solution.py:527
  12.9 1.0 %shard_map.141 = (f32[64,128]{1,0:T(8,128)}, f32[64,1024]{1,0:T(8,128)}) custom-call(f32[64,128]{1,0:T(8,128)S(1)} %get-tuple-element.8.merged, f32[64,1024]{1,0:T(8,128)S(1)} %get-tuple-element.9.base, bf16[256,1024]{1,0:T(8,128)(2,1)S(1)} %get-tuple-element.10.patch_of, f32[128,128]{1,0:T(8,128)S(1)} %get-tuple-element.11.answers), custom_call_target="tpu_custom_call" | custom-call | tf_op jit(solution)/shard_map/pallas_call | solution.py:561

commit v6 on v5

--- a/solution.py
+++ b/solution.py
@@ -88,10 +88,10 @@
 ):
     count_ref, *refs = refs
     sources, refs = refs[:INPUTS], refs[INPUTS:]
-    merged_ref, base_ref, patch_of_ref, answers_ref = refs[:4]
-    tables, own, ask, asked, note, noted, fore, reply, back, send, recv = refs[4:15]
-    send_sem, recv_sem, in_sem, known = refs[15:19]
-    staged = refs[19:]
+    got_ref, owned_of_ref, frac_out, other_ref, base_ref, patch_of_ref, answers_ref = refs[:7]
+    tables, own, ask, asked, note, noted, fore, reply, back, send, recv = refs[7:18]
+    send_sem, recv_sem, in_sem, known = refs[18:22]
+    staged = refs[22:]
     (
         target_ref, lwt_ref, lgrid_ref, clu_ref, cwt_ref, pcol_ref, pwt_ref,
         scale_ref, pft_ref, flux_ref,
@@ -417,7 +417,8 @@
         slabs(respond_rest)
         back[0] = reply[keeper]
 
-    other = (1.0 - frac) * field_ref[...]
+    other_ref[...] = (1.0 - frac) * field_ref[...]
+    frac_out[...] = frac
     pair, side = split_by(entry, 2)
     answers = outer_clump * pairs * slots
     spot = side * answers + (slab * pairs + pair) * slots + rank
@@ -446,7 +447,7 @@
     ids_of = jnp.broadcast_to(told.reshape(n, stride, 128)[:, 0:1, :], (n, stride, 128)).reshape(rows, 128)
     spread = jnp.where(its_lane, jnp.concatenate([ids_of, ids_of], axis=0), 0.0).astype(BF16)
     ids = dot(spread, jnp.ones((128, cells), BF16))
-    owned_of = onehot(ids == (iota((2 * rows, cells), 1) + 1).astype(F32))
+    owned_of_ref[...] = onehot(ids == (iota((2 * rows, cells), 1) + 1).astype(F32))
 
     back_of = (table * outer_clump + behind(my_slab, to_slab, outer_clump)) * inner_group
     back_of = (back_of + behind(my_core, to_core, inner_group)) * stride + 1
@@ -460,25 +461,25 @@
     def _():
         wait(reply.at[pl.ds(0, askers - 1)], send_sem.at[1])
 
-    wait(recv.at[flat], recv_sem.at[2])
-    in_half = split_by(iota((rows, 128), 0), stride)[1] < half
-    owned = select(unpack(jnp.where(in_half, recv[...], 0.0)), owned_of)
-    merged_ref[...] = frac * owned + other
-
     for which, first in keeps_or_not:
 
         @pl.when(which)
         def _(first=first):
             wait(back.at[pl.ds(first, outer_clump - first)], recv_sem.at[3])
 
+    wait(recv.at[flat], recv_sem.at[2])
+    in_half = split_by(iota((rows, 128), 0), stride)[1] < half
+    got_ref[...] = jnp.where(in_half, recv[...], 0.0)
     answers_ref[...] = back[...].reshape(answers, 128)
 
 
-def store_kernel(merged, base, patch_of, answers, merged_out, anomaly_out, anomaly, sem):
+def store_kernel(
+    got, owned_of, frac, other, base, patch_of, answers,
+    merged_out, anomaly_out, merged, anomaly, sem,
+):
     chunks = anomaly.shape[0]
     width = anomaly.shape[2]
-    stores = [pltpu.make_async_copy(merged, merged_out, sem.at[chunks])]
-    stores[0].start()
+    stores = []
     high, low = halves(unpack(answers[...]))
     table = jnp.concatenate([high, low], axis=0)
     for k in range(chunks):
@@ -487,6 +488,9 @@
         anomaly[k] = base[:, its] - (both[: high.shape[0]] + both[high.shape[0] :])
         stores.append(pltpu.make_async_copy(anomaly.at[k], anomaly_out.at[:, its], sem.at[k]))
         stores[-1].start()
+    merged[...] = frac[...] * select(unpack(got[...]), owned_of[...]) + other[...]
+    stores.append(pltpu.make_async_copy(merged, merged_out, sem.at[chunks]))
+    stores[-1].start()
     for store in stores:
         store.wait()
 
@@ -529,13 +533,16 @@
             kernel, n_clump, n_group, inner_clump, inner_group, cap, slots, half, stride
         ),
         out_shape=(
+            pltpu.VMEM((n * stride, 128), F32),
+            pltpu.VMEM((2 * n * stride, cells), BF16),
+            pltpu.VMEM((1, cells), F32),
             pltpu.VMEM((nv, cells), F32),
             pltpu.VMEM((nv, patches), F32),
             pltpu.VMEM((2 * answers, patches), BF16),
             pltpu.VMEM((answers, 128), F32),
         ),
         in_specs=[pl.BlockSpec(memory_space=pltpu.SMEM)] + [hbm] * INPUTS,
-        out_specs=(vmem,) * 4,
+        out_specs=(vmem,) * 7,
         scratch_shapes=[
             pltpu.VMEM((sharers, -(-(nv + 1) // 8) * 8, cells), F32),
             pltpu.VMEM((-(-(nv + 1) // 8) * 8, cells), F32),
@@ -561,9 +568,10 @@
     merged, anomaly = pl.pallas_call(
         store_kernel,
         out_shape=shapes,
-        in_specs=[vmem] * 4,
+        in_specs=[vmem] * 7,
         out_specs=(hbm, hbm),
         scratch_shapes=[
+            pltpu.VMEM((nv, cells), F32),
             pltpu.VMEM((chunks, nv, patches // chunks), F32),
             pltpu.SemaphoreType.DMA((chunks + 1,)),
         ],

time: 14.1 us -> 13.9 us (0.986)
  no operation moved by 1% of the time
where the time goes in v6:
time: 13.9 us; the launch traced here: 13.8 us
  Pallas kernels  12.5 us (90%)
  between operations  1.29 us (9%)
    pallas_call x1, Pallas kernels, per_device(): pl.pallas_call(functools.partial(kernel, n_clump, n_group, inner_clump, i...  11.5 us
    pallas_call x1, Pallas kernels, per_device(): pl.pallas_call(store_kernel, out_shape=shapes, in_specs=[vmem] * 7, out_s...  0.99 us

profile of v6, /device:TPU:0, one launch (start us, length us, event | category | flops | bytes accessed | tf_op | source)
XLA Modules:
  0.0 13.8 jit_solution(12438546291838150954)
XLA Ops:
  1.3 11.5 %shard_map.140 = (f32[256,128]{1,0:T(8,128)S(1)}, bf16[512,128]{1,0:T(8,128)(2,1)S(1)}, f32[1,128]{1,0:T(1,128)S(1)}, f32[64,128]{1,0:T(8,128)S(1)}, f32[64,1024...) custom-call(s32[1]{0:T(128)S(6)} %copy.15.refs_0_, s32[1,128]{1,0:T(1,128)} %refs_1_.1, ...), custom_call_target="tpu_custom_call" | custom-call | tf_op jit(solution)/shard_map/pallas_call | solution.py:531
  12.8 1.0 %shard_map.141 = (f32[64,128]{1,0:T(8,128)}, f32[64,1024]{1,0:T(8,128)}) custom-call(f32[256,128]{1,0:T(8,128)S(1)} %get-tuple-element.11.got, bf16[512,128]{1,0:T(8,128)(2,1)S(1)} %get-tuple-element.12.owned_of, f32[1,128]{1,0:T(1,128)S(1)} %get-tuple-element.13.frac, f32[64,128]{1,0:T(8,128)S(1)} %get-tuple-element.14.other, ...), custom_call_target="tpu_custom_call" | custom-call | tf_op jit(solution)/shard_map/pallas_call | solution.py:568

commit v7 on v6

--- a/solution.py
+++ b/solution.py
@@ -180,6 +180,11 @@
 
         offsets(one, inner_clump, outer_group, far_first=True)
 
+    def against(block):
+        o, i = block // outer_group, block % outer_group
+        row, side = ahead_of(my_row, o, inner_clump), ahead_of(my_side, i, outer_group)
+        return (row >= my_row) & (side >= my_side), (row <= my_row) & (side <= my_side)
+
     def slabs(act):
         if outer_clump <= 8:
             for o in range(1, outer_clump):
@@ -202,9 +207,13 @@
     last_chip = last_place & last_plane
     last = last_chip & keeps
 
-    def greet(step, device):
-        for core in range(inner_group):
-            signal(barrier, core_of(device, core))
+    def greet(block, device):
+        signal(barrier, keeper_of(device))
+
+        @pl.when(against(block)[0])
+        def _():
+            for core in range(keeper):
+                signal(barrier, core_of(device, core))
 
     @pl.when(keeps)
     def _():
@@ -226,31 +235,41 @@
 
     table_rows = pl.ds(0, nv + 1)
 
-    def share(block, device):
-        into = tables.at[block * inner_group + my_core, table_rows]
-        remote(own.at[table_rows], into, 0, keeper_of(device))
-
-    def enter():
+    def share(block, device, direct=False):
+        at = block * inner_group + my_core
+        if direct:
+            remote(sources[11], tables.at[at, pl.ds(0, nv)], 0, keeper_of(device))
+            remote(sources[10], tables.at[at, pl.ds(nv, 1)], 0, keeper_of(device))
+        else:
+            remote(own.at[table_rows], tables.at[at, table_rows], 0, keeper_of(device))
+
+    def get_own():
         loads[10].wait()
         loads[11].wait()
-        near = places - 1 + jnp.where(keeps, outer_clump - 1 + keeper, 1)
+
+    def enter_keeper():
+        get_own()
+        near = places - 1 + outer_clump - 1 + keeper
         pl.semaphore_wait(barrier, jnp.where(last, n - 1, near))
         each_place(share, ahead_of)
-
-        @pl.when(keeps)
-        def _():
-            for core in range(keeper):
-                signal(known.at[0], core_of(here, core))
-
-        @pl.when(jnp.logical_not(keeps))
-        def _():
-            share(0, here)
+        for core in range(keeper):
+            signal(known.at[0], core_of(here, core))
 
         @pl.when(last)
         def _():
             each_other(lambda block, device: signal(known.at[1], device), ahead_of)
 
-    pl.when(last_chip)(enter)
+    def enter_other(direct):
+        pl.semaphore_wait(barrier, (my_row + 1) * (my_side + 1))
+
+        def share_lower(block, device):
+            pl.when(against(block)[1])(lambda: share(block, device, direct))
+
+        each_place(share_lower, ahead_of)
+        share(0, here, direct)
+
+    pl.when(last)(enter_keeper)
+    pl.when(last_chip & jnp.logical_not(keeps))(lambda: enter_other(True))
     loads[0].wait()
     target = target_ref[...]
     owner, local = split_by(target, cells)
@@ -271,7 +290,9 @@
     for k in range(outer_clump):
         ask[k, 0:1, :] = ask_rows[k : k + 1]
     one_row = pl.ds(0, 1)
-    pl.when(jnp.logical_not(last_chip))(enter)
+    pl.when(keeps & jnp.logical_not(last))(enter_keeper)
+    pl.when(jnp.logical_not(keeps))(get_own)
+    pl.when(jnp.logical_not(keeps | last_chip))(lambda: enter_other(False))
 
     def request(step, device):
         into = asked.at[step * inner_group + my_core, one_row]
@@ -284,6 +305,11 @@
     @pl.when(jnp.logical_not(keeps))
     def _():
         pl.semaphore_wait(known.at[0], 1)
+
+        def share_rest(block, device):
+            pl.when(jnp.logical_not(against(block)[1]))(lambda: share(block, device))
+
+        each_place(share_rest, ahead_of)
 
     each_slab(request, ahead_of)
     frac = frac_ref[...]

time: 13.9 us -> 14.2 us (1.022)
  Pallas kernels: 12.5 us -> 12.7 us
    pallas_call x1, Pallas kernels: 11.5 us -> 11.7 us  [per_device(): pl.pallas_call(functools.partial(kernel, n_clump, n_group, inner_clump, i...]
where the time goes in v7:
time: 14.2 us; the launch traced here: 14 us
  Pallas kernels  12.7 us (89%)
  between operations  1.29 us (9%)
    pallas_call x1, Pallas kernels, per_device(): pl.pallas_call(functools.partial(kernel, n_clump, n_group, inner_clump, i...  11.7 us
    pallas_call x1, Pallas kernels, per_device(): pl.pallas_call(store_kernel, out_shape=shapes, in_specs=[vmem] * 7, out_s...  0.98 us

profile of v7, /device:TPU:0, one launch (start us, length us, event | category | flops | bytes accessed | tf_op | source)
XLA Modules:
  0.0 14.0 jit_solution(14159312484714615054)
XLA Ops:
  1.3 11.7 %shard_map.140 = (f32[256,128]{1,0:T(8,128)S(1)}, bf16[512,128]{1,0:T(8,128)(2,1)S(1)}, f32[1,128]{1,0:T(1,128)S(1)}, f32[64,128]{1,0:T(8,128)S(1)}, f32[64,1024...) custom-call(s32[1]{0:T(128)S(6)} %copy.15.refs_0_, s32[1,128]{1,0:T(1,128)} %refs_1_.1, ...), custom_call_target="tpu_custom_call" | custom-call | tf_op jit(solution)/shard_map/pallas_call | solution.py:557
  13.0 1.0 %shard_map.141 = (f32[64,128]{1,0:T(8,128)}, f32[64,1024]{1,0:T(8,128)}) custom-call(f32[256,128]{1,0:T(8,128)S(1)} %get-tuple-element.11.got, bf16[512,128]{1,0:T(8,128)(2,1)S(1)} %get-tuple-element.12.owned_of, f32[1,128]{1,0:T(1,128)S(1)} %get-tuple-element.13.frac, f32[64,128]{1,0:T(8,128)S(1)} %get-tuple-element.14.other, ...), custom_call_target="tpu_custom_call" | custom-call | tf_op jit(solution)/shard_map/pallas_call | solution.py:594
